TPU v7x, 64 devices: a 2x2x8 block of a 4x4x8 slice. The times are simulated.
64 devices in a mesh: dp: 4 (over x, y), sp: 16 (over z, core).
Axes of the slice: x: 2, y: 2, z: 8, core: 2. Of those that a mesh axis runs over, the one named last changes fastest.
The devices are a block of a 4x4x8 slice.
Arguments:
- hidden: bfloat16 [512, 6144], P('dp'), parts along dimension 0
- w_norm: bfloat16 [6144], replicated
- w_q: bfloat16 [6144, 6144], replicated
- w_k: bfloat16 [6144, 128], replicated
- w_v: bfloat16 [6144, 128], replicated
- w_o: bfloat16 [6144, 6144], replicated
- k_cache: bfloat16 [512, 2048, 128], P('dp', 'sp'), parts along dimension 0
- v_cache: bfloat16 [512, 2048, 128], P('dp', 'sp'), parts along dimension 0
- cache_len: int32 [512], P('dp'), parts along dimension 0
Outputs:
- output 1: bfloat16 [512, 6144], P('dp'), parts along dimension 0
- output 2: bfloat16 [512, 2048, 128], P('dp', 'sp'), parts along dimension 0
- output 3: bfloat16 [512, 2048, 128], P('dp', 'sp'), parts along dimension 0
There are 4 independent parts. A program takes and returns all parts, laid end to end along the dimension named above; an argument that names none is the same for every part.
All inputs are finite; a program needn't handle non-finite values.
Results may differ from a plain program's by a relative error of at most 0.0151788.
Values sent between devices are 32-bit elements.
A program may use at most 768 MiB of HBM per device.

v0:
```python
import jax
import jax.numpy as jnp
from jax import lax
from jax.sharding import PartitionSpec as P

ROPE_BASE = 10000.0
EPSILON = 1e-6


def rotate_half(vectors, cos_t, sin_t):
    half_dim = vectors.shape[-1] // 2
    lower_half = vectors[..., :half_dim]
    upper_half = vectors[..., half_dim:]
    return jnp.concatenate([lower_half * cos_t - upper_half * sin_t, upper_half * cos_t + lower_half * sin_t], axis=-1)


def project_token(hidden, w_norm, w_q, w_k, w_v, cache_len):
    head_dim = w_k.shape[1]
    num_heads = w_q.shape[1] // head_dim
    num_rows = hidden.shape[0]
    x_f32 = hidden.astype(jnp.float32)
    inv_rms = lax.rsqrt(jnp.mean(x_f32 * x_f32, axis=-1, keepdims=True) + EPSILON)
    x_norm = (x_f32 * inv_rms * (1.0 + w_norm.astype(jnp.float32))).astype(jnp.bfloat16)
    q_proj = jnp.dot(x_norm, w_q, preferred_element_type=jnp.float32).astype(jnp.bfloat16)
    k_proj = jnp.dot(x_norm, w_k, preferred_element_type=jnp.float32).astype(jnp.bfloat16)
    v_proj = jnp.dot(x_norm, w_v, preferred_element_type=jnp.float32).astype(jnp.bfloat16)
    inv_freq = ROPE_BASE ** (-jnp.arange(head_dim // 2, dtype=jnp.float32) * 2.0 / head_dim)
    angles = cache_len.astype(jnp.float32)[:, None] * inv_freq[None, :]
    cos_t = jnp.cos(angles)
    sin_t = jnp.sin(angles)
    q_heads = q_proj.astype(jnp.float32).reshape(num_rows, num_heads, head_dim)
    q_rot = (rotate_half(q_heads, cos_t[:, None, :], sin_t[:, None, :]) * head_dim ** -0.5).astype(jnp.bfloat16)
    k_rot = rotate_half(k_proj.astype(jnp.float32), cos_t, sin_t).astype(jnp.bfloat16)
    return x_f32, q_rot, k_rot, v_proj


def local_step(hidden, w_norm, w_q, w_k, w_v, w_o, k_block, v_block, cache_len):
    num_rows = hidden.shape[0]
    seq_block = k_block.shape[1]
    x_f32, q_rot, k_rot, v_proj = project_token(hidden, w_norm, w_q, w_k, w_v, cache_len)
    positions = lax.axis_index('sp') * seq_block + jnp.arange(seq_block)
    at_slot = (positions[None, :] == cache_len[:, None])[:, :, None]
    new_k_block = jnp.where(at_slot, k_rot[:, None, :], k_block)
    new_v_block = jnp.where(at_slot, v_proj[:, None, :], v_block)
    is_valid = (positions[None, :] <= cache_len[:, None])[:, None, :]
    scores = jnp.einsum('rhd,rtd->rht', q_rot, new_k_block, preferred_element_type=jnp.float32)
    masked = jnp.where(is_valid, scores, -jnp.inf)
    row_max = lax.pmax(jnp.max(masked, axis=-1), 'sp')
    weights = jnp.exp(masked - row_max[:, :, None])
    part_num = jnp.einsum('rht,rtd->rhd', weights.astype(jnp.bfloat16), new_v_block, preferred_element_type=jnp.float32)
    part_den = jnp.sum(weights, axis=-1)
    numerator, denominator = lax.psum((part_num, part_den), 'sp')
    attended = (numerator / denominator[:, :, None]).astype(jnp.bfloat16).reshape(num_rows, -1)
    out_hidden = x_f32 + jnp.dot(attended, w_o, preferred_element_type=jnp.float32)
    return out_hidden.astype(jnp.bfloat16), new_k_block, new_v_block


def solution(mesh):
    cache_spec = P('dp', 'sp', None)
    return jax.shard_map(local_step, mesh=mesh, in_specs=(P('dp', None), P(None), P(None, None), P(None, None), P(None, None), P(None, None), cache_spec, cache_spec, P('dp')), out_specs=(P('dp', None), cache_spec, cache_spec), check_vma=False)
```

profile of v0, /device:TPU:21, one launch (start us, length us, event | category | flops | bytes accessed | tf_op | source)
XLA Modules:
  0.0 265.5 jit_solution(15392745351654011327)
XLA Ops:
  7.2 0.0 copy-start
  7.2 0.0 copy-start.2
  7.2 0.1 all-reduce.2.cloned.1.call-start
  7.3 0.0 copy-start.5
  7.3 0.8 convert_element_type.46
  8.1 2.3 fusion.2
  10.4 0.7 convert_add_fusion
  11.1 0.7 broadcast_compare_fusion.1
  11.9 0.0 copy-done
  11.9 2.1 convolution_convert_fusion.1
  14.0 0.9 fusion.19
  14.9 0.2 multiply_cosine_fusion
  15.1 0.1 copy.12
  15.2 0.1 copy.14
  15.3 0.1 copy.13
  15.4 28.0 %fusion.8 = f32[16,8,48,128]{3,1,2,0:T(8,128)} fusion(bf16[6144,6144]{1,0:T(8,128)(2,1)} %param.11, bf16[128,6144]{1,0:T(8,128)(2,1)S(1)} %copy-done.2, f32[6144]{0:T(1024)S(1)} %convert_add_fusion, f32[128]{0:T(128)S(1)} %add_rsqrt_fusion), kind=kOutput, calls=%fused_computation.20 | convolution fusion | flops 9668395008 | bytes 80241152 | tf_op jit(solution)/shard_map/dot_general | solution.py:24
  43.4 2.4 copy.15
  45.8 0.0 copy-start.3
  45.8 0.0 copy-start.4
  45.9 1.1 multiply_subtract_fusion
  46.9 1.1 copy-done.3
  48.0 1.3 copy-done.4
  49.3 4.9 %broadcast_select_fusion.1 = (bf16[128,128,128]{2,1,0:T(8,128)(2,1)S(1)}, bf16[128,128,128]{2,1,0:T(8,128)(2,1)}) fusion(bf16[128,128,128]{2,1,0:T(8,128)(2,1)S(1)} %copy-done.3, pred[128,128]{1,0:T(8,128)(4,1)S(1)} %get-tuple-element.10, bf16[128,128]{1,0:T(8,128)(2,1)S(1)} %copy.14, bf16[128,128,128]{2,1,0:T(8,128)(2,1)S(1)} %copy-done.4, ...), kind=kLoop, calls=%fused_computation.7 | loop fusion | flops 4194304 | bytes 16859136 | tf_op jit(solution)/shard_map/jit(_where)/select_n | solution.py:43
  54.2 4.8 %select_reduce_fusion = (f32[128,48]{1,0:T(8,128)S(1)}, f32[128,48,128]{2,1,0:T(8,128)}) fusion(pred[128,128]{1,0:T(8,128)(4,1)S(1)} %get-tuple-element.9, bf16[128,128,128]{2,1,0:T(8,128)(2,1)S(1)} %get-tuple-element.7, f32[128,48,64]{2,1,0:T(8,128)S(1)} %get-tuple-element.4, f32[128,48,64]{2,1,0:T(8,128)S(1)} %get-tuple-element.3), kind=kOutput, calls=%fused_computation.17 | convolution fusion | flops 205252608 | bytes 10526720 | tf_op jit(solution)/shard_map/rhd,rtd->rht/dot_general | solution.py:46
  59.0 50.3 %pmax.7 = f32[128,48]{1,0:T(8,128)S(1)} all-reduce(f32[128,48]{1,0:T(8,128)S(1)} %get-tuple-element.15), channel_id=1, replica_groups=mesh['dp'=4,'sp'=16] {'sp'}, use_global_device_ids=true, to_apply=%region_2.3 | all-reduce | flops 6144 | bytes 49152 | tf_op jit(solution)/shard_map/pmax | solution.py:48
  109.4 6.1 %fusion.9 = f32[128,48,128]{2,1,0:T(8,128)} fusion(bf16[128,128,128]{2,1,0:T(8,128)(2,1)} %get-tuple-element.8, f32[128,48,128]{2,1,0:T(8,128)} %get-tuple-element.16, f32[128,48]{1,0:T(8,128)S(1)} %pmax.7, pred[128,128]{1,0:T(8,128)(4,1)S(1)} %get-tuple-element.9), kind=kOutput, calls=%fused_computation.21 | convolution fusion | flops 203685888 | bytes 10526720 | tf_op jit(solution)/shard_map/rht,rtd->rhd/dot_general | solution.py:50
  115.5 0.1 all-reduce.2.cloned.1.call-update
  115.6 3.2 %fusion.6 = f32[128,48]{1,0:T(8,128)S(1)} fusion(f32[128,48,128]{2,1,0:T(8,128)} %get-tuple-element.16, f32[128,48]{1,0:T(8,128)S(1)} %pmax.7, pred[128,128]{1,0:T(8,128)(4,1)S(1)} %get-tuple-element.9), kind=kLoop, calls=%fused_computation.18 | loop fusion | flops 2353152 | bytes 3211264 | tf_op jit(solution)/shard_map/reduce_sum | solution.py:51
  118.8 46.0 %psum.15 = f32[128,48]{1,0:T(8,128)S(1)} all-reduce(f32[128,48]{1,0:T(8,128)S(1)} %fusion.6), channel_id=1, replica_groups=mesh['dp'=4,'sp'=16] {'sp'}, use_global_device_ids=true, to_apply=%region_5.6 | all-reduce | flops 6144 | bytes 49152 | tf_op jit(solution)/shard_map/psum | solution.py:52
  164.8 62.8 %all-reduce.2.cloned.1.call-done = f32[128,48,128]{2,1,0:T(8,128)} async-done(((f32[128,48,128]{2,1,0:T(8,128)}), f32[128,48,128]{2,1,0:T(8,128)}) %all-reduce.2.cloned.1.call-update) | async-done | bytes 3145744 | tf_op jit(solution)/shard_map/psum | solution.py:52
  227.6 3.3 %divide_convert_fusion = bf16[128,48,128]{2,1,0:T(8,128)(2,1)} fusion(f32[128,48,128]{2,1,0:T(8,128)} %all-reduce.2.cloned.1.call-done, f32[128,48]{1,0:T(8,128)S(1)} %psum.15), kind=kLoop, calls=%fused_computation.13 | loop fusion | flops 1572864 | bytes 4743168 | tf_op jit(solution)/shard_map/convert_element_type | solution.py:53
  230.9 27.8 %fusion = bf16[128,6144]{1,0:T(8,128)(2,1)} fusion(bf16[6144,6144]{1,0:T(8,128)(2,1)} %param.14, bf16[128,6144]{1,0:T(8,128)(2,1)S(1)} %copy-done.2, bf16[16,8,48,128]{3,2,1,0:T(8,128)(2,1)} %bitcast.14), kind=kOutput, calls=%fused_computation.1 | convolution fusion | flops 9666035712 | bytes 80216064 | tf_op jit(solution)/shard_map/dot_general | solution.py:54
  (8 shorter events, 0.0 us)
Async XLA Ops:
  7.2 4.7 %copy-start = (bf16[6144,128]{1,0:T(8,128)(2,1)S(1)}, bf16[6144,128]{1,0:T(8,128)(2,1)}, u32[]{:S(2)}) copy-start(bf16[6144,128]{1,0:T(8,128)(2,1)} %param.13) | copy-start | bytes 4718596
  7.2 6.8 %copy-start.2 = (bf16[128,6144]{1,0:T(8,128)(2,1)S(1)}, bf16[128,6144]{1,0:T(8,128)(2,1)}, u32[]{:S(2)}) copy-start(bf16[128,6144]{1,0:T(8,128)(2,1)} %param.9) | copy-start | bytes 4718596
  7.2 220.4 %all-reduce.2.cloned.1.call-start = ((), (), s32[]{:S(2)}) async-start(), calls=%async_computation | async-start | bytes 6291456 | tf_op jit(solution)/shard_map/psum | solution.py:52
  7.3 6.7 %copy-start.5 = (bf16[6144,128]{1,0:T(8,128)(2,1)S(1)}, bf16[6144,128]{1,0:T(8,128)(2,1)}, u32[]{:S(2)}) copy-start(bf16[6144,128]{1,0:T(8,128)(2,1)} %param.12) | copy-start | bytes 4718596
  45.8 2.2 copy-start.3
  45.8 3.5 %copy-start.4 = (bf16[128,128,128]{2,1,0:T(8,128)(2,1)S(1)}, bf16[128,128,128]{2,1,0:T(8,128)(2,1)}, u32[]{:S(2)}) copy-start(bf16[128,128,128]{2,1,0:T(8,128)(2,1)} %param.16) | copy-start | bytes 12582916
  54.2 4.8 %copy-start.1 = (bf16[128,128,128]{2,1,0:T(8,128)(2,1)}, bf16[128,128,128]{2,1,0:T(8,128)(2,1)S(1)}, u32[]{:S(2)}) copy-start(bf16[128,128,128]{2,1,0:T(8,128)(2,1)S(1)} %get-tuple-element.7) | copy-start | bytes 12582916
Sparse Core Ops, SparseCore 0:
  115.7 111.8 all-reduce.1
where the time goes:
time: 266 us
  blocking collectives  96.4 us (36%)
  matrix products  69.7 us (26%)
  waiting for transfers between devices  62.8 us (24%)
  other arithmetic  17.2 us (6%)
  between operations  14.2 us (5%)
  local copies, waits for them, and re-layouts  5.16 us (2%)
    psum x1, waiting for transfers between devices, local_step(): numerator, denominator = lax.psum((part_num, part_den), 'sp')  62.8 us
    pmax x1, blocking collectives, local_step(): row_max = lax.pmax(jnp.max(masked, axis=-1), 'sp')  50.3 us
    psum x1, blocking collectives, local_step(): numerator, denominator = lax.psum((part_num, part_den), 'sp')  46 us
    dot_general x1, matrix products, project_token(): jnp.dot(x_norm, w_q, preferred_element_type=jnp.float32)  28 us
    dot_general x1, matrix products, local_step(): jnp.dot(attended, w_o, preferred_element_type=jnp.float32)  27.8 us
    dot_general x1, matrix products, local_step(): jnp.einsum('rht,rtd->rhd', weights.astype(jnp.bfloat16), new_v_block, pre...  6.15 us
  transfers between devices with their start and end apart: 1, of which 1 were waited for; matrix products, arithmetic and copies ran while one was open for 1% of the time, Pallas kernels for 0%

commit v1 on v0

v1 whole, which is shorter than its diff:
```python
import functools

import jax
import jax.numpy as jnp
import numpy as np
from jax import lax
from jax.experimental import pallas as pl
from jax.experimental.pallas import tpu as pltpu
from jax.sharding import PartitionSpec as P

ROPE_BASE = 10000.0
EPSILON = 1e-6
MIB = 1024 * 1024
F32 = jnp.float32
BF16 = jnp.bfloat16
FLOOR = float(np.finfo(np.float32).min)
MESH = pl.DeviceIdType.MESH
ROW_BLOCK = 8
PROJ_SLOTS = 4
OUT_SLOTS = 4
OUT_TILE = 512


def remote(src, dst, send_sem, recv_sem, device):
    return pltpu.make_async_remote_copy(src_ref=src, dst_ref=dst, send_sem=send_sem, recv_sem=recv_sem, device_id={'sp': device}, device_id_type=MESH)


def enter(devices):
    barrier = pltpu.get_barrier_semaphore()
    for device in devices:
        pl.semaphore_signal(barrier, inc=1, device_id={'sp': device}, device_id_type=MESH)
    pl.semaphore_wait(barrier, len(devices))


def project_kernel(x_ref, w_norm_ref, cos_ref, sin_ref, w_q_ref, w_k_ref, w_v_ref, q_ref, k_ref, v_ref, x_norm, w_buf, w_sem, kv_sem, send_sem, recv_sem):
    me = lax.axis_index('sp')
    core = me % 2
    partner = me + 1 - 2 * core
    num_rows, width = x_ref.shape
    head = k_ref.shape[1]
    half = q_ref.shape[0] // 2
    pair = 2 * head
    num_blocks = half // 2
    first_head = core * half

    def fetch(block):
        slot = (block + 1) % PROJ_SLOTS
        columns = pl.ds(pl.multiple_of((first_head + 2 * block) * head, pair), pair)
        return pltpu.make_async_copy(w_q_ref.at[:, columns], w_buf.at[slot], w_sem.at[slot])

    fetch_k = pltpu.make_async_copy(w_k_ref, w_buf.at[0, :, pl.ds(0, head)], kv_sem.at[0])
    fetch_v = pltpu.make_async_copy(w_v_ref, w_buf.at[0, :, pl.ds(head, head)], kv_sem.at[1])
    fetch_k.start()
    fetch_v.start()
    for block in range(PROJ_SLOTS - 1):
        fetch(block).start()

    gain = 1.0 + w_norm_ref[...].astype(F32)

    def normalise(step, carry):
        rows = pl.ds(pl.multiple_of(step * 16, 16), 16)
        x = x_ref[rows, :].astype(F32)
        inv_rms = lax.rsqrt(jnp.mean(x * x, axis=-1, keepdims=True) + EPSILON)
        x_norm[rows, :] = (x * inv_rms * gain).astype(BF16)
        return carry

    lax.fori_loop(0, num_rows // 16, normalise, 0)
    cos_t = cos_ref[...]
    sin_t = sin_ref[...]

    def rotate(u):
        u = u.astype(BF16).astype(F32)
        return u * cos_t + pltpu.roll(u, head // 2, 1) * sin_t

    fetch_k.wait()
    fetch_v.wait()
    both = jnp.dot(x_norm[...], w_buf[0], preferred_element_type=F32)
    k_ref[...] = rotate(both[:, :head]).astype(BF16).astype(F32)
    v_ref[...] = both[:, head:].astype(BF16).astype(F32)
    fetch(PROJ_SLOTS - 1).start()
    enter([partner])

    def send(block):
        heads = q_ref.at[pl.ds(first_head + 2 * block, 2)]
        return remote(heads, heads, send_sem.at[block], recv_sem.at[block], partner)

    def step(block, carry):
        fetch(block).wait()
        product = jnp.dot(x_norm[...], w_buf[(block + 1) % PROJ_SLOTS], preferred_element_type=F32)

        @pl.when(block + PROJ_SLOTS < num_blocks)
        def _():
            fetch(block + PROJ_SLOTS).start()

        for i in range(2):
            q_ref[first_head + 2 * block + i] = (rotate(product[:, i * head:(i + 1) * head]) * head ** -0.5).astype(BF16).astype(F32)
        send(block).start()
        return carry

    lax.fori_loop(0, num_blocks, step, 0)

    def finish(block, carry):
        other = q_ref.at[pl.ds((1 - core) * half + 2 * block, 2)]
        remote(other, other, send_sem.at[block], recv_sem.at[block], partner).wait_recv()
        send(block).wait_send()
        return carry

    lax.fori_loop(0, num_blocks, finish, 0)


def project(hidden, w_norm, w_q, w_k, w_v, cache_len):
    num_rows, width = hidden.shape
    head = w_k.shape[1]
    heads = w_q.shape[1] // head
    inv_freq = jnp.asarray(ROPE_BASE ** (-np.arange(head // 2) * 2.0 / head), F32)
    angles = cache_len.astype(F32)[:, None] * jnp.concatenate([inv_freq, inv_freq])[None, :]
    sign = jnp.asarray(np.where(np.arange(head) < head // 2, -1.0, 1.0), F32)
    vmem = pl.BlockSpec(memory_space=pltpu.VMEM)
    hbm = pl.BlockSpec(memory_space=pl.ANY)
    blocks = heads // 4
    return pl.pallas_call(
        project_kernel,
        name='project',
        out_shape=(jax.ShapeDtypeStruct((heads, num_rows, head), F32), jax.ShapeDtypeStruct((num_rows, head), F32), jax.ShapeDtypeStruct((num_rows, head), F32)),
        in_specs=[vmem, vmem, vmem, vmem, hbm, hbm, hbm],
        out_specs=(vmem, vmem, vmem),
        scratch_shapes=[
            pltpu.VMEM((num_rows, width), BF16),
            pltpu.VMEM((PROJ_SLOTS, width, 2 * head), BF16),
            pltpu.SemaphoreType.DMA((PROJ_SLOTS,)),
            pltpu.SemaphoreType.DMA((2,)),
            pltpu.SemaphoreType.DMA((blocks,)),
            pltpu.SemaphoreType.DMA((blocks,)),
        ],
        compiler_params=pltpu.CompilerParams(collective_id=0, has_side_effects=True, vmem_limit_bytes=40 * MIB),
    )(hidden, w_norm.reshape(1, -1), jnp.cos(angles), jnp.sin(angles) * sign, w_q, w_k, w_v)


def attend_kernel(len_ref, q_ref, k_new_ref, v_new_ref, k_ref, v_ref, k_out, v_out, num_ref, stat_ref, staged):
    heads, rows, head = q_ref.shape
    slots = k_ref.shape[1]
    base = lax.axis_index('sp') * slots
    queries = q_ref.reshape(heads * rows, head)
    group_iota = lax.broadcasted_iota(jnp.int32, (16, head), 0)
    lane_iota = lax.broadcasted_iota(jnp.int32, (heads, slots), 1)
    for r in range(rows):
        row = pl.program_id(0) * rows + r
        p = len_ref[row] - base
        group = pl.multiple_of(jnp.clip(p, 0, slots - 1) // 16 * 16, 16)
        for new, old, out in ((k_new_ref, k_ref, k_out), (v_new_ref, v_ref, v_out)):
            out[r] = old[r]
            tile = old[r, pl.ds(group, 16), :].astype(F32)
            out[r, pl.ds(group, 16), :] = jnp.where(group_iota == p - group, new[r:r + 1, :], tile).astype(BF16)
        q = queries[pl.ds(r, heads, stride=rows), :].astype(BF16)
        scores = lax.dot_general(q, k_out[r], (((1,), (1,)), ((), ())), preferred_element_type=F32)
        valid = lane_iota <= p
        scores = jnp.where(valid, scores, FLOOR)
        row_max = jnp.max(scores, axis=1, keepdims=True)
        weights = jnp.where(valid, jnp.exp(scores - row_max), 0.0)
        total = jnp.sum(weights, axis=1, keepdims=True)
        staged[pl.ds(r, heads, stride=rows), :] = jnp.dot(weights.astype(BF16), v_out[r], preferred_element_type=F32)
        here = lane_iota == row
        stat_ref[0:heads, :] = jnp.where(here, row_max, stat_ref[0:heads, :])
        stat_ref[heads:2 * heads, :] = jnp.where(here, total, stat_ref[heads:2 * heads, :])
    num_ref[...] = staged[...].reshape(heads, rows, head)


def attend(q, k_new, v_new, k_block, v_block, cache_len):
    heads, num_rows, head = q.shape
    slots = k_block.shape[1]
    rows = ROW_BLOCK
    by_head = pl.BlockSpec((heads, rows, head), lambda i, *_: (0, i, 0))
    by_row = pl.BlockSpec((rows, head), lambda i, *_: (i, 0))
    cache = pl.BlockSpec((rows, slots, head), lambda i, *_: (i, 0, 0))
    stats = pl.BlockSpec((2 * heads, num_rows), lambda i, *_: (0, 0))
    return pl.pallas_call(
        attend_kernel,
        name='attend',
        out_shape=(jax.ShapeDtypeStruct(k_block.shape, BF16), jax.ShapeDtypeStruct(v_block.shape, BF16), jax.ShapeDtypeStruct(q.shape, F32), jax.ShapeDtypeStruct((2 * heads, num_rows), F32)),
        grid_spec=pltpu.PrefetchScalarGridSpec(
            num_scalar_prefetch=1,
            grid=(num_rows // rows,),
            in_specs=[by_head, by_row, by_row, cache, cache],
            out_specs=(cache, cache, by_head, stats),
            scratch_shapes=[pltpu.VMEM((heads * rows, head), F32)],
        ),
        compiler_params=pltpu.CompilerParams(dimension_semantics=('arbitrary',), vmem_limit_bytes=32 * MIB),
    )(cache_len, q, k_new, v_new, k_block, v_block)


def combine_kernel(nz, num_ref, stat_ref, x_ref, w_o_ref, out_ref, near_num, near_stat, part, from_long, from_short, gathered, total, attended, w_buf, w_sem, stat_sem, near_send, near_recv, long_send, long_recv, short_send, short_recv, far_send, far_recv, back_send, back_recv, side_send, side_recv):
    me = lax.axis_index('sp')
    z = me // 2
    core = me % 2
    partner = me + 1 - 2 * core
    way = 1 - 2 * core
    heads, num_rows, head = num_ref.shape
    share = heads // (2 * nz)
    far = nz // 2
    width = out_ref.shape[1]
    depth = 2 * share * head

    def device(chip, c):
        return (chip + 2 * nz) % nz * 2 + c

    ahead = device(z + way, core)
    behind = device(z - way, core)
    targets = [far]
    for hop in range(far - 1, 0, -1):
        targets += [-hop, hop]
    targets.append(0)
    sources = [0]
    for hop in range(1, far):
        sources += [-hop, hop]
    sources.append(-far)

    def fetch(k):
        chip = device(z + way * sources[k], 0) // 2
        return pltpu.make_async_copy(w_o_ref.at[pl.ds(pl.multiple_of(chip * depth, depth), depth), :], w_buf.at[k % OUT_SLOTS], w_sem.at[k % OUT_SLOTS])

    for k in range(OUT_SLOTS):
        fetch(k).start()
    enter([partner, ahead, behind])

    swap_stat = remote(stat_ref, near_stat, stat_sem.at[0], stat_sem.at[1], partner)
    swap_stat.start()
    swaps = []
    for i, hop in enumerate(targets):
        first = share * device(z - way * hop, 1 - core)
        swap = remote(num_ref.at[pl.ds(first, share)], near_num.at[i], near_send.at[i], near_recv.at[i], partner)
        swap.start()
        swaps.append(swap)

    def column(row):
        return jnp.broadcast_to(row, (num_rows, num_rows)).T

    def merge(a, b):
        (x_a, m_a, l_a), (x_b, m_b, l_b) = a, b
        m = jnp.maximum(m_a, m_b)
        scale_a = jnp.exp(m_a - m)
        scale_b = jnp.exp(m_b - m)
        return x_a * column(scale_a) + x_b * column(scale_b), m, l_a * scale_a + l_b * scale_b

    def load(ref):
        return ref[0:num_rows, :], ref[num_rows:num_rows + 1, :], ref[num_rows + 1:num_rows + 2, :]

    sub_iota = lax.broadcasted_iota(jnp.int32, (8, num_rows), 0)

    def store(ref, triple):
        x, m, l = triple
        ref[0:num_rows, :] = x
        ref[num_rows:num_rows + 8, :] = jnp.where(sub_iota == 0, m, l)

    def own(i):
        swaps[i].wait_recv()
        first = share * device(z + way * targets[i], core)
        for s in range(share):
            h = first + s
            mine = (num_ref[h], stat_ref[pl.ds(h, 1), :], stat_ref[pl.ds(heads + h, 1), :])
            theirs = (near_num[i, s], near_stat[pl.ds(h, 1), :], near_stat[pl.ds(heads + h, 1), :])
            store(part.at[i, s], merge(mine, theirs))

    def long_copy(hop, s):
        i = 0 if hop == 0 else 2 * hop
        return remote(part.at[i, s], from_long.at[hop, s], long_send.at[hop, s], long_recv.at[hop, s], ahead)

    def short_copy(hop, s):
        return remote(part.at[2 * hop + 1, s], from_short.at[hop, s], short_send.at[hop, s], short_recv.at[hop, s], behind)

    swap_stat.wait_recv()
    for hop in range(far):
        own(2 * hop)
        if hop == 0:
            for s in range(share):
                long_copy(0, s).start()
        own(2 * hop + 1)
        if hop == 0:
            for s in range(share):
                short_copy(0, s).start()
            continue
        for s in range(share):
            long_copy(hop - 1, s).wait_recv()
            store(part.at[2 * hop, s], merge(load(part.at[2 * hop, s]), load(from_long.at[hop - 1, s])))
            long_copy(hop, s).start()
            if hop < far - 1:
                short_copy(hop - 1, s).wait_recv()
                store(part.at[2 * hop + 1, s], merge(load(part.at[2 * hop + 1, s]), load(from_short.at[hop - 1, s])))
                short_copy(hop, s).start()

    def far_copy(hop, s):
        slot = gathered.at[device(z - way * hop, core), s]
        return remote(slot, slot, far_send.at[hop, s], far_recv.at[hop, s], ahead)

    def back_copy(hop, s):
        slot = gathered.at[device(z + way * hop, core), s]
        return remote(slot, slot, back_send.at[hop, s], back_recv.at[hop, s], behind)

    def side_copy(k, s):
        slot = gathered.at[device(z + way * sources[k], core), s]
        return remote(slot, slot, side_send.at[k, s], side_recv.at[k, s], partner)

    def far_arrival(hop, s):
        slot = gathered.at[device(z - way * (hop + 1), core), s]
        return remote(slot, slot, far_send.at[hop, s], far_recv.at[hop, s], ahead)

    def back_arrival(hop, s):
        slot = gathered.at[device(z + way * (hop + 1), core), s]
        return remote(slot, slot, back_send.at[hop, s], back_recv.at[hop, s], behind)

    def side_arrival(k, s):
        slot = gathered.at[device(z - way * sources[k], 1 - core), s]
        return remote(slot, slot, side_send.at[k, s], side_recv.at[k, s], partner)

    mirror = {hop: k for k, hop in enumerate(sources)}
    mirror[far] = mirror[-far]

    last = far - 1
    for s in range(share):
        short_copy(last - 1, s).wait_recv()
        triple = merge(load(part.at[2 * far - 1, s]), load(from_short.at[last - 1, s]))
        long_copy(last, s).wait_recv()
        x, _, l = merge(triple, load(from_long.at[last, s]))
        gathered[me, s] = (x / column(l)).astype(BF16).astype(F32)
        far_copy(0, s).start()
        back_copy(0, s).start()
        side_copy(0, s).start()

    tiles = width // OUT_TILE

    def prepare(k):
        for s in range(share):
            side_arrival(mirror[-sources[k]], s).wait_recv()
        chip = z + way * sources[k]
        for c in range(2):
            for s in range(share):
                attended[:, (c * share + s) * head:(c * share + s + 1) * head] = gathered[device(chip, c), s].astype(BF16)
        fetch(k).wait()

    def multiply(k, low, high):
        def tile(n, carry):
            columns = pl.ds(pl.multiple_of(n * OUT_TILE, OUT_TILE), OUT_TILE)
            product = jnp.dot(attended[...], w_buf[k % OUT_SLOTS, :, columns], preferred_element_type=F32)
            if k == 0:
                total[:, columns] = product
            elif k < nz - 1:
                total[:, columns] = total[:, columns] + product
            else:
                out_ref[:, columns] = (x_ref[:, columns].astype(F32) + (total[:, columns] + product)).astype(BF16)
            return carry

        lax.fori_loop(low, high, tile, 0)
        if high == tiles and k + OUT_SLOTS < nz:
            fetch(k + OUT_SLOTS).start()

    pending = [0]
    for hop in range(far):
        work = [(k, n) for k in pending for n in range(2)]
        for s in range(share):
            far_arrival(hop, s).wait_recv()
            if hop < far - 1:
                far_copy(hop + 1, s).start()
            side_copy(mirror[-(hop + 1)], s).start()
            if hop < far - 1:
                back_arrival(hop, s).wait_recv()
                if hop < far - 2:
                    back_copy(hop + 1, s).start()
                side_copy(mirror[hop + 1], s).start()
            count = -(-len(work) // (share - s))
            for k, n in work[:count]:
                if n == 0:
                    prepare(k)
                multiply(k, n * tiles // 2, (n + 1) * tiles // 2)
            work = work[count:]
        pending = [mirror[-(hop + 1)]] + ([mirror[hop + 1]] if hop < far - 1 else [])
    for k in pending:
        prepare(k)
        multiply(k, 0, tiles)

    swap_stat.wait_send()
    for swap in swaps:
        swap.wait_send()
    for s in range(share):
        for hop in range(far):
            long_copy(hop, s).wait_send()
            far_copy(hop, s).wait_send()
            if hop < far - 1:
                short_copy(hop, s).wait_send()
                back_copy(hop, s).wait_send()
        for k in range(nz):
            side_copy(k, s).wait_send()


def combine(num, stat, hidden, w_o, group):
    heads, num_rows, head = num.shape
    nz = group // 2
    share = heads // group
    far = nz // 2
    width = w_o.shape[1]
    vmem = pl.BlockSpec(memory_space=pltpu.VMEM)
    hbm = pl.BlockSpec(memory_space=pl.ANY)
    dma = pltpu.SemaphoreType.DMA
    piece = (num_rows + 8, head)
    return pl.pallas_call(
        functools.partial(combine_kernel, nz),
        name='combine',
        out_shape=jax.ShapeDtypeStruct((num_rows, width), BF16),
        in_specs=[vmem, vmem, vmem, hbm],
        out_specs=vmem,
        scratch_shapes=[
            pltpu.VMEM((nz, share, num_rows, head), F32),
            pltpu.VMEM((2 * heads, num_rows), F32),
            pltpu.VMEM((nz, share) + piece, F32),
            pltpu.VMEM((far, share) + piece, F32),
            pltpu.VMEM((far - 1, share) + piece, F32),
            pltpu.VMEM((group, share, num_rows, head), F32),
            pltpu.VMEM((num_rows, width), F32),
            pltpu.VMEM((num_rows, 2 * share * head), BF16),
            pltpu.VMEM((OUT_SLOTS, 2 * share * head, width), BF16),
            dma((OUT_SLOTS,)),
            dma((2,)),
            dma((nz,)),
            dma((nz,)),
            dma((far, share)),
            dma((far, share)),
            dma((far - 1, share)),
            dma((far - 1, share)),
            dma((far, share)),
            dma((far, share)),
            dma((far - 1, share)),
            dma((far - 1, share)),
            dma((nz, share)),
            dma((nz, share)),
        ],
        compiler_params=pltpu.CompilerParams(collective_id=1, has_side_effects=True, vmem_limit_bytes=62 * MIB),
    )(num, stat, hidden, w_o)


def solution(mesh):
    group = mesh.shape['sp']

    def local_step(hidden, w_norm, w_q, w_k, w_v, w_o, k_block, v_block, cache_len):
        q, k_new, v_new = project(hidden, w_norm, w_q, w_k, w_v, cache_len)
        k_out, v_out, num, stat = attend(q, k_new, v_new, k_block, v_block, cache_len)
        out = combine(num, stat, hidden, w_o, group)
        return out, k_out, v_out

    cache_spec = P('dp', 'sp', None)
    return jax.shard_map(local_step, mesh=mesh, in_specs=(P('dp', None), P(None), P(None, None), P(None, None), P(None, None), P(None, None), cache_spec, cache_spec, P('dp')), out_specs=(P('dp', None), cache_spec, cache_spec), check_vma=False)
```

time: 266 us -> 126 us (0.47)
  Pallas kernels: 0 us -> 114 us
  blocking collectives: 96.4 us -> 0 us
  matrix products: 69.7 us -> 0 us
  waiting for transfers between devices: 62.8 us -> 0 us
  other arithmetic: 17.2 us -> 1.64 us
  between operations: 14.2 us -> 0.69 us
  local copies, waits for them, and re-layouts: 5.16 us -> 9.89 us
    pallas_call x0 -> x3, Pallas kernels: none -> 114 us  [the longest x1 60 us: combine(): pl.pallas_call(functools.partial(combine_kernel, nz), name='combine', out...]
    dot_general x6 -> x0, matrix products: 69.7 us -> none  [the longest x1 28 us: project_token(): jnp.dot(x_norm, w_q, preferred_element_type=jnp.float32)]
    psum x1 -> x0, waiting for transfers between devices: 62.8 us -> none  [local_step(): numerator, denominator = lax.psum((part_num, part_den), 'sp')]
    pmax x1 -> x0, blocking collectives: 50.3 us -> none  [local_step(): row_max = lax.pmax(jnp.max(masked, axis=-1), 'sp')]
    psum x1 -> x0, blocking collectives: 46 us -> none  [local_step(): numerator, denominator = lax.psum((part_num, part_den), 'sp')]
    reduce_sum x2 -> x0, other arithmetic: 5.49 us -> none  [the longest x1 3.22 us: local_step(): part_den = jnp.sum(weights, axis=-1)]
    select_n x1 -> x0, other arithmetic: 4.88 us -> none  [local_step(): new_k_block = jnp.where(at_slot, k_rot[:, None, :], k_block)]
    unnamed x13 -> x17, local copies, waits for them, and re-layouts: 4.86 us -> 9.17 us
  transfers between devices with their start and end apart: 1 -> 0, of which waited for: 1 -> 0; matrix products, arithmetic and copies ran while one was open for 1% -> 0% of each run, Pallas kernels for 0% -> 0%
where the time goes in v1:
time: 126 us
  Pallas kernels  114 us (90%)
  local copies, waits for them, and re-layouts  9.89 us (8%)
  other arithmetic  1.64 us (1%)
    pallas_call x1, Pallas kernels, combine(): pl.pallas_call(functools.partial(combine_kernel, nz), name='combine', out...  60 us
    pallas_call x1, Pallas kernels, attend(): pl.pallas_call(attend_kernel, name='attend', out_shape=(jax.ShapeDtypeStr...  34.5 us
    pallas_call x1, Pallas kernels, project(): pl.pallas_call(project_kernel, name='project', out_shape=(jax.ShapeDtypeS...  19.5 us
    unnamed x17, local copies, waits for them, and re-layouts  9.17 us

profile of v1, /device:TPU:21, one launch (start us, length us, event | category | flops | bytes accessed | tf_op | source)
XLA Modules:
  0.0 126.2 jit_solution(4476762911447962164)
XLA Ops:
  0.6 0.7 convert_element_type.3
  1.3 0.7 reshape.12.w_norm_ref
  2.0 1.0 fusion
  3.0 0.0 copy-start
  3.0 1.4 %copy-done = bf16[128,6144]{1,0:T(8,128)(2,1)S(1)} copy-done((bf16[128,6144]{1,0:T(8,128)(2,1)S(1)}, bf16[128,6144]{1,0:T(8,128)(2,1)}, u32[]{:S(2)}) %copy-start) | copy-done | bytes 1572888
  4.4 0.0 copy-start.4
  4.4 1.4 %copy-done.4 = bf16[6144,128]{1,0:T(8,128)(2,1)S(1)} copy-done((bf16[6144,128]{1,0:T(8,128)(2,1)S(1)}, bf16[6144,128]{1,0:T(8,128)(2,1)}, u32[]{:S(2)}) %copy-start.4) | copy-done | bytes 1572888
  5.8 0.0 copy-start.5
  5.8 1.4 %copy-done.5 = bf16[6144,128]{1,0:T(8,128)(2,1)S(1)} copy-done((bf16[6144,128]{1,0:T(8,128)(2,1)S(1)}, bf16[6144,128]{1,0:T(8,128)(2,1)}, u32[]{:S(2)}) %copy-start.5) | copy-done | bytes 1572888
  7.2 0.0 copy-start.1
  7.2 0.0 copy-start.2
  7.2 0.0 copy-start.7
  7.2 19.5 %project.1 = (f32[48,128,128]{2,1,0:T(8,128)S(1)}, f32[128,128]{1,0:T(8,128)S(1)}, f32[128,128]{1,0:T(8,128)S(1)}) custom-call(bf16[128,6144]{1,0:T(8,128)(2,1)S(1)} %copy-done, bf16[1,6144]{1,0:T(2,128)(2,1)S(1)} %reshape.12.w_norm_ref, f32[128,128]{1,0:T(8,128)S(1)} %get-tuple-element.18.cos_ref, f32[128,128]{1,0:T(8,128)S(1)} %get-tuple-element.17.sin_ref, ...), custom_call_target="tpu_custom_call" | custom-call | tf_op jit(solution)/shard_map/project/pallas_call | solution.py:121
  26.7 0.0 copy-done.1
  26.7 0.0 copy-done.2
  26.7 0.0 copy-done.7
  26.7 34.5 %attend.1 = (bf16[128,128,128]{2,1,0:T(8,128)(2,1)}, bf16[128,128,128]{2,1,0:T(8,128)(2,1)}, f32[48,128,128]{2,1,0:T(8,128)S(1)}, f32[96,128]{1,0:T(8,128)S(1)}) custom-call(s32[128]{0:T(128)S(1)} %copy-done.7, f32[48,128,128]{2,1,0:T(8,128)S(1)} %get-tuple-element.10.q_ref, f32[128,128]{1,0:T(8,128)S(1)} %get-tuple-element.11.k_new_ref, ...), custom_call_target="tpu_custom_call" | custom-call | tf_op jit(solution)/shard_map/attend/pallas_call | solution.py:176
  61.2 0.0 copy-start.3
  61.2 1.6 %copy-done.3 = f32[48,128,128]{2,1,0:T(8,128)} copy-done((f32[48,128,128]{2,1,0:T(8,128)}, f32[48,128,128]{2,1,0:T(8,128)S(1)}, u32[]{:S(2)}) %copy-start.3) | copy-done | bytes 3145752
  62.8 0.0 copy-start.6
  62.8 0.6 copy-done.6
  63.5 60.0 %combine.1 = bf16[128,6144]{1,0:T(8,128)(2,1)} custom-call(f32[48,128,128]{2,1,0:T(8,128)} %copy-done.3, f32[96,128]{1,0:T(8,128)} %copy-done.6, bf16[128,6144]{1,0:T(8,128)(2,1)} %x_ref.3, bf16[6144,6144]{1,0:T(8,128)(2,1)} %w_o_ref.1), custom_call_target="tpu_custom_call" | custom-call | tf_op jit(solution)/shard_map/combine/pallas_call | solution.py:403
  123.5 2.7 %copy.15 = bf16[128,6144]{1,0:T(8,128)(2,1)} copy(bf16[128,6144]{1,0:T(8,128)(2,1)} %combine.1) | data formatting | bytes 3145728
Async XLA Ops:
  3.0 1.4 %copy-start = (bf16[128,6144]{1,0:T(8,128)(2,1)S(1)}, bf16[128,6144]{1,0:T(8,128)(2,1)}, u32[]{:S(2)}) copy-start(bf16[128,6144]{1,0:T(8,128)(2,1)} %x_ref.3) | copy-start | bytes 4718596
  4.4 1.4 %copy-start.4 = (bf16[6144,128]{1,0:T(8,128)(2,1)S(1)}, bf16[6144,128]{1,0:T(8,128)(2,1)}, u32[]{:S(2)}) copy-start(bf16[6144,128]{1,0:T(8,128)(2,1)} %w_k_ref.1) | copy-start | bytes 4718596
  5.8 1.4 %copy-start.5 = (bf16[6144,128]{1,0:T(8,128)(2,1)S(1)}, bf16[6144,128]{1,0:T(8,128)(2,1)}, u32[]{:S(2)}) copy-start(bf16[6144,128]{1,0:T(8,128)(2,1)} %w_v_ref.1) | copy-start | bytes 4718596
  7.2 19.5 %copy-start.1 = (bf16[128,128,128]{2,1,0:T(8,128)(2,1)S(1)}, bf16[128,128,128]{2,1,0:T(8,128)(2,1)}, u32[]{:S(2)}) copy-start(bf16[128,128,128]{2,1,0:T(8,128)(2,1)} %k_ref.1) | copy-start | bytes 12582916
  7.2 19.5 %copy-start.2 = (bf16[128,128,128]{2,1,0:T(8,128)(2,1)S(1)}, bf16[128,128,128]{2,1,0:T(8,128)(2,1)}, u32[]{:S(2)}) copy-start(bf16[128,128,128]{2,1,0:T(8,128)(2,1)} %v_ref.1) | copy-start | bytes 12582916
  7.2 19.5 %copy-start.7 = (s32[128]{0:T(128)S(1)}, s32[128]{0:T(128)}, u32[]{:S(2)}) copy-start(s32[128]{0:T(128)} %len_ref.1) | copy-start | bytes 1540
  61.2 1.6 %copy-start.3 = (f32[48,128,128]{2,1,0:T(8,128)}, f32[48,128,128]{2,1,0:T(8,128)S(1)}, u32[]{:S(2)}) copy-start(f32[48,128,128]{2,1,0:T(8,128)S(1)} %get-tuple-element.13.num_ref) | copy-start | bytes 9437188
  62.8 0.6 copy-start.6

commit v2 on v1

--- a/solution.py
+++ b/solution.py
@@ -15,10 +15,11 @@
 BF16 = jnp.bfloat16
 FLOOR = float(np.finfo(np.float32).min)
 MESH = pl.DeviceIdType.MESH
+TURN = (6.28125, 0.0019340515136718750, float(2 * np.pi - 6.28125 - 0.0019340515136718750))
 ROW_BLOCK = 8
 PROJ_SLOTS = 4
 OUT_SLOTS = 4
-OUT_TILE = 512
+OUT_TILE = 1536
 
 
 def remote(src, dst, send_sem, recv_sem, device):
@@ -32,13 +33,13 @@
     pl.semaphore_wait(barrier, len(devices))
 
 
-def project_kernel(x_ref, w_norm_ref, cos_ref, sin_ref, w_q_ref, w_k_ref, w_v_ref, q_ref, k_ref, v_ref, x_norm, w_buf, w_sem, kv_sem, send_sem, recv_sem):
+def project_kernel(freq_ref, len_ref, w_norm_ref, x_hbm, w_q_ref, w_k_ref, w_v_ref, q_ref, k_ref, v_ref, x_ref, x_norm, w_buf, q_buf, x_sem, w_sem, kv_sem, out_sem, send_sem, recv_sem):
     me = lax.axis_index('sp')
     core = me % 2
     partner = me + 1 - 2 * core
     num_rows, width = x_ref.shape
     head = k_ref.shape[1]
-    half = q_ref.shape[0] // 2
+    half = q_ref.shape[1] // ROW_BLOCK // 2
     pair = 2 * head
     num_blocks = half // 2
     first_head = core * half
@@ -50,12 +51,21 @@
 
     fetch_k = pltpu.make_async_copy(w_k_ref, w_buf.at[0, :, pl.ds(0, head)], kv_sem.at[0])
     fetch_v = pltpu.make_async_copy(w_v_ref, w_buf.at[0, :, pl.ds(head, head)], kv_sem.at[1])
+    fetch_x = pltpu.make_async_copy(x_hbm, x_ref, x_sem.at[0])
+    fetch_x.start()
     fetch_k.start()
     fetch_v.start()
     for block in range(PROJ_SLOTS - 1):
         fetch(block).start()
 
     gain = 1.0 + w_norm_ref[...].astype(F32)
+    angles = jnp.broadcast_to(len_ref[...].astype(F32), (num_rows, num_rows)).T * freq_ref[...]
+    turns = jnp.round(angles * (0.5 / np.pi))
+    for part in TURN:
+        angles = angles - turns * part
+    cos_t = jnp.cos(angles)
+    sin_t = jnp.where(lax.broadcasted_iota(jnp.int32, angles.shape, 1) < head // 2, -1.0, 1.0) * jnp.sin(angles)
+    fetch_x.wait()
 
     def normalise(step, carry):
         rows = pl.ds(pl.multiple_of(step * 16, 16), 16)
@@ -65,8 +75,6 @@
         return carry
 
     lax.fori_loop(0, num_rows // 16, normalise, 0)
-    cos_t = cos_ref[...]
-    sin_t = sin_ref[...]
 
     def rotate(u):
         u = u.astype(BF16).astype(F32)
@@ -80,9 +88,15 @@
     fetch(PROJ_SLOTS - 1).start()
     enter([partner])
 
+    def heads_of(c, block):
+        rows = pl.multiple_of((c * half + 2 * block) * ROW_BLOCK, 2 * ROW_BLOCK)
+        return q_ref.at[:, pl.ds(rows, 2 * ROW_BLOCK), :]
+
+    def keep(block):
+        return pltpu.make_async_copy(q_buf.at[block], heads_of(core, block), out_sem.at[block])
+
     def send(block):
-        heads = q_ref.at[pl.ds(first_head + 2 * block, 2)]
-        return remote(heads, heads, send_sem.at[block], recv_sem.at[block], partner)
+        return remote(q_buf.at[block], heads_of(core, block), send_sem.at[block], recv_sem.at[block], partner)
 
     def step(block, carry):
         fetch(block).wait()
@@ -93,16 +107,19 @@
             fetch(block + PROJ_SLOTS).start()
 
         for i in range(2):
-            q_ref[first_head + 2 * block + i] = (rotate(product[:, i * head:(i + 1) * head]) * head ** -0.5).astype(BF16).astype(F32)
+            q = (rotate(product[:, i * head:(i + 1) * head]) * head ** -0.5).astype(BF16).astype(F32)
+            q_buf[block, :, i * ROW_BLOCK:(i + 1) * ROW_BLOCK, :] = q.reshape(num_rows // ROW_BLOCK, ROW_BLOCK, head)
         send(block).start()
+        keep(block).start()
         return carry
 
     lax.fori_loop(0, num_blocks, step, 0)
 
     def finish(block, carry):
-        other = q_ref.at[pl.ds((1 - core) * half + 2 * block, 2)]
-        remote(other, other, send_sem.at[block], recv_sem.at[block], partner).wait_recv()
+        keep(block).wait()
         send(block).wait_send()
+        other = heads_of(1 - core, block)
+        remote(q_buf.at[block], other, send_sem.at[block], recv_sem.at[block], partner).wait_recv()
         return carry
 
     lax.fori_loop(0, num_blocks, finish, 0)
@@ -112,64 +129,76 @@
     num_rows, width = hidden.shape
     head = w_k.shape[1]
     heads = w_q.shape[1] // head
-    inv_freq = jnp.asarray(ROPE_BASE ** (-np.arange(head // 2) * 2.0 / head), F32)
-    angles = cache_len.astype(F32)[:, None] * jnp.concatenate([inv_freq, inv_freq])[None, :]
-    sign = jnp.asarray(np.where(np.arange(head) < head // 2, -1.0, 1.0), F32)
+    inv_freq = ROPE_BASE ** (-np.arange(head // 2) * 2.0 / head)
+    inv_freq = jnp.asarray(np.concatenate([inv_freq, inv_freq])[None, :], F32)
     vmem = pl.BlockSpec(memory_space=pltpu.VMEM)
-    hbm = pl.BlockSpec(memory_space=pl.ANY)
+    hbm = pl.BlockSpec(memory_space=pltpu.HBM)
     blocks = heads // 4
     return pl.pallas_call(
         project_kernel,
         name='project',
-        out_shape=(jax.ShapeDtypeStruct((heads, num_rows, head), F32), jax.ShapeDtypeStruct((num_rows, head), F32), jax.ShapeDtypeStruct((num_rows, head), F32)),
-        in_specs=[vmem, vmem, vmem, vmem, hbm, hbm, hbm],
-        out_specs=(vmem, vmem, vmem),
+        out_shape=(jax.ShapeDtypeStruct((num_rows // ROW_BLOCK, heads * ROW_BLOCK, head), F32), jax.ShapeDtypeStruct((num_rows, head), F32), jax.ShapeDtypeStruct((num_rows, head), F32)),
+        in_specs=[vmem, vmem, vmem, hbm, hbm, hbm, hbm],
+        out_specs=(hbm, vmem, vmem),
         scratch_shapes=[
             pltpu.VMEM((num_rows, width), BF16),
+            pltpu.VMEM((num_rows, width), BF16),
             pltpu.VMEM((PROJ_SLOTS, width, 2 * head), BF16),
+            pltpu.VMEM((blocks, num_rows // ROW_BLOCK, 2 * ROW_BLOCK, head), F32),
+            pltpu.SemaphoreType.DMA((1,)),
             pltpu.SemaphoreType.DMA((PROJ_SLOTS,)),
             pltpu.SemaphoreType.DMA((2,)),
             pltpu.SemaphoreType.DMA((blocks,)),
             pltpu.SemaphoreType.DMA((blocks,)),
+            pltpu.SemaphoreType.DMA((blocks,)),
         ],
-        compiler_params=pltpu.CompilerParams(collective_id=0, has_side_effects=True, vmem_limit_bytes=40 * MIB),
-    )(hidden, w_norm.reshape(1, -1), jnp.cos(angles), jnp.sin(angles) * sign, w_q, w_k, w_v)
-
-
-def attend_kernel(len_ref, q_ref, k_new_ref, v_new_ref, k_ref, v_ref, k_out, v_out, num_ref, stat_ref, staged):
-    heads, rows, head = q_ref.shape
-    slots = k_ref.shape[1]
+        compiler_params=pltpu.CompilerParams(collective_id=0, has_side_effects=True, vmem_limit_bytes=60 * MIB),
+    )(inv_freq, cache_len.reshape(1, -1), w_norm, hidden, w_q, w_k, w_v)
+
+
+def attend_kernel(len_ref, q_ref, k_new_ref, v_new_ref, k_ref, v_ref, k_out, v_out, num_ref, stat_ref, scores_ref):
+    rows, slots, head = k_ref.shape
+    heads = stat_ref.shape[0] // 2
     base = lax.axis_index('sp') * slots
-    queries = q_ref.reshape(heads * rows, head)
+    first = pl.program_id(0) * rows
     group_iota = lax.broadcasted_iota(jnp.int32, (16, head), 0)
     lane_iota = lax.broadcasted_iota(jnp.int32, (heads, slots), 1)
-    for r in range(rows):
-        row = pl.program_id(0) * rows + r
-        p = len_ref[row] - base
-        group = pl.multiple_of(jnp.clip(p, 0, slots - 1) // 16 * 16, 16)
-        for new, old, out in ((k_new_ref, k_ref, k_out), (v_new_ref, v_ref, v_out)):
-            out[r] = old[r]
+    places = [len_ref[first + r] - base for r in range(rows)]
+    for new, old, out in ((k_new_ref, k_ref, k_out), (v_new_ref, v_ref, v_out)):
+        out[...] = old[...]
+        for r, p in enumerate(places):
+            group = pl.multiple_of(jnp.clip(p, 0, slots - 1) // 16 * 16, 16)
             tile = old[r, pl.ds(group, 16), :].astype(F32)
             out[r, pl.ds(group, 16), :] = jnp.where(group_iota == p - group, new[r:r + 1, :], tile).astype(BF16)
-        q = queries[pl.ds(r, heads, stride=rows), :].astype(BF16)
-        scores = lax.dot_general(q, k_out[r], (((1,), (1,)), ((), ())), preferred_element_type=F32)
+    for r in range(rows):
+        q = q_ref[pl.ds(r, heads, stride=rows), :].astype(BF16)
+        scores_ref[r] = lax.dot_general(q, k_out[r], (((1,), (1,)), ((), ())), preferred_element_type=F32)
+    maxima, totals, factors = [], [], []
+    for r, p in enumerate(places):
         valid = lane_iota <= p
-        scores = jnp.where(valid, scores, FLOOR)
+        scores = jnp.where(valid, scores_ref[r], FLOOR)
         row_max = jnp.max(scores, axis=1, keepdims=True)
         weights = jnp.where(valid, jnp.exp(scores - row_max), 0.0)
-        total = jnp.sum(weights, axis=1, keepdims=True)
-        staged[pl.ds(r, heads, stride=rows), :] = jnp.dot(weights.astype(BF16), v_out[r], preferred_element_type=F32)
-        here = lane_iota == row
-        stat_ref[0:heads, :] = jnp.where(here, row_max, stat_ref[0:heads, :])
-        stat_ref[heads:2 * heads, :] = jnp.where(here, total, stat_ref[heads:2 * heads, :])
-    num_ref[...] = staged[...].reshape(heads, rows, head)
+        maxima.append(row_max)
+        totals.append(jnp.sum(weights, axis=1, keepdims=True))
+        factors.append(weights.astype(BF16))
+    for r in range(rows):
+        num_ref[pl.ds(r, heads, stride=rows), :] = jnp.dot(factors[r], v_out[r], preferred_element_type=F32)
+    stat_m = stat_ref[0:heads, :]
+    stat_l = stat_ref[heads:2 * heads, :]
+    for r in range(rows):
+        here = lane_iota == first + r
+        stat_m = jnp.where(here, maxima[r], stat_m)
+        stat_l = jnp.where(here, totals[r], stat_l)
+    stat_ref[0:heads, :] = stat_m
+    stat_ref[heads:2 * heads, :] = stat_l
 
 
 def attend(q, k_new, v_new, k_block, v_block, cache_len):
-    heads, num_rows, head = q.shape
-    slots = k_block.shape[1]
+    num_rows, slots, head = k_block.shape
     rows = ROW_BLOCK
-    by_head = pl.BlockSpec((heads, rows, head), lambda i, *_: (0, i, 0))
+    heads = q.shape[1] // rows
+    by_head = pl.BlockSpec((None, heads * rows, head), lambda i, *_: (i, 0, 0))
     by_row = pl.BlockSpec((rows, head), lambda i, *_: (i, 0))
     cache = pl.BlockSpec((rows, slots, head), lambda i, *_: (i, 0, 0))
     stats = pl.BlockSpec((2 * heads, num_rows), lambda i, *_: (0, 0))
@@ -182,22 +211,23 @@
             grid=(num_rows // rows,),
             in_specs=[by_head, by_row, by_row, cache, cache],
             out_specs=(cache, cache, by_head, stats),
-            scratch_shapes=[pltpu.VMEM((heads * rows, head), F32)],
+            scratch_shapes=[pltpu.VMEM((rows, heads, slots), F32)],
         ),
-        compiler_params=pltpu.CompilerParams(dimension_semantics=('arbitrary',), vmem_limit_bytes=32 * MIB),
+        compiler_params=pltpu.CompilerParams(dimension_semantics=('arbitrary',), vmem_limit_bytes=60 * MIB),
     )(cache_len, q, k_new, v_new, k_block, v_block)
 
 
-def combine_kernel(nz, num_ref, stat_ref, x_ref, w_o_ref, out_ref, near_num, near_stat, part, from_long, from_short, gathered, total, attended, w_buf, w_sem, stat_sem, near_send, near_recv, long_send, long_recv, short_send, short_recv, far_send, far_recv, back_send, back_recv, side_send, side_recv):
+def combine_kernel(nz, stat_ref, num_ref, x_hbm, w_o_ref, out_hbm, x_ref, out_ref, own_num, near_num, near_stat, part, from_long, from_short, gathered, total, attended, w_buf, x_sem, out_sem, own_sem, w_sem, stat_sem, near_send, near_recv, long_send, long_recv, short_send, short_recv, far_send, far_recv, back_send, back_recv, side_send, side_recv):
     me = lax.axis_index('sp')
     z = me // 2
     core = me % 2
     partner = me + 1 - 2 * core
     way = 1 - 2 * core
-    heads, num_rows, head = num_ref.shape
+    num_rows, width = x_ref.shape
+    heads = num_ref.shape[1] // ROW_BLOCK
+    head = num_ref.shape[2]
     share = heads // (2 * nz)
     far = nz // 2
-    width = out_ref.shape[1]
     depth = 2 * share * head
 
     def device(chip, c):
@@ -218,18 +248,27 @@
         chip = device(z + way * sources[k], 0) // 2
         return pltpu.make_async_copy(w_o_ref.at[pl.ds(pl.multiple_of(chip * depth, depth), depth), :], w_buf.at[k % OUT_SLOTS], w_sem.at[k % OUT_SLOTS])
 
-    for k in range(OUT_SLOTS):
-        fetch(k).start()
+    def own_heads(i, c):
+        way_c = way * (1 - 2 * c)
+        rows = share * ROW_BLOCK
+        first = rows * device(z + way_c * targets[i], core + way * c)
+        return num_ref.at[:, pl.ds(pl.multiple_of(first, rows), rows), :]
+
+    own_copies = [pltpu.make_async_copy(own_heads(i, 0), own_num.at[i], own_sem.at[i]) for i in range(nz)]
+    for copy in own_copies:
+        copy.start()
     enter([partner, ahead, behind])
-
     swap_stat = remote(stat_ref, near_stat, stat_sem.at[0], stat_sem.at[1], partner)
     swap_stat.start()
     swaps = []
-    for i, hop in enumerate(targets):
-        first = share * device(z - way * hop, 1 - core)
-        swap = remote(num_ref.at[pl.ds(first, share)], near_num.at[i], near_send.at[i], near_recv.at[i], partner)
+    for i in range(nz):
+        swap = remote(own_heads(i, 1), near_num.at[i], near_send.at[i], near_recv.at[i], partner)
         swap.start()
         swaps.append(swap)
+    fetch_x = pltpu.make_async_copy(x_hbm, x_ref, x_sem.at[0])
+    fetch_x.start()
+    for k in range(OUT_SLOTS):
+        fetch(k).start()
 
     def column(row):
         return jnp.broadcast_to(row, (num_rows, num_rows)).T
@@ -252,12 +291,13 @@
         ref[num_rows:num_rows + 8, :] = jnp.where(sub_iota == 0, m, l)
 
     def own(i):
+        own_copies[i].wait()
         swaps[i].wait_recv()
         first = share * device(z + way * targets[i], core)
         for s in range(share):
             h = first + s
-            mine = (num_ref[h], stat_ref[pl.ds(h, 1), :], stat_ref[pl.ds(heads + h, 1), :])
-            theirs = (near_num[i, s], near_stat[pl.ds(h, 1), :], near_stat[pl.ds(heads + h, 1), :])
+            mine = (own_num[i, :, s * ROW_BLOCK:(s + 1) * ROW_BLOCK, :].reshape(num_rows, head), stat_ref[pl.ds(h, 1), :], stat_ref[pl.ds(heads + h, 1), :])
+            theirs = (near_num[i, :, s * ROW_BLOCK:(s + 1) * ROW_BLOCK, :].reshape(num_rows, head), near_stat[pl.ds(h, 1), :], near_stat[pl.ds(heads + h, 1), :])
             store(part.at[i, s], merge(mine, theirs))
 
     def long_copy(hop, s):
@@ -327,34 +367,43 @@
 
     tiles = width // OUT_TILE
 
-    def prepare(k):
-        for s in range(share):
-            side_arrival(mirror[-sources[k]], s).wait_recv()
-        chip = z + way * sources[k]
-        for c in range(2):
+    def save(n):
+        columns = pl.ds(pl.multiple_of(n * OUT_TILE, OUT_TILE), OUT_TILE)
+        return pltpu.make_async_copy(out_ref.at[:, columns], out_hbm.at[:, columns], out_sem.at[n])
+
+    def prepare(ks):
+        for i, k in enumerate(ks):
             for s in range(share):
-                attended[:, (c * share + s) * head:(c * share + s + 1) * head] = gathered[device(chip, c), s].astype(BF16)
-        fetch(k).wait()
-
-    def multiply(k, low, high):
-        def tile(n, carry):
-            columns = pl.ds(pl.multiple_of(n * OUT_TILE, OUT_TILE), OUT_TILE)
-            product = jnp.dot(attended[...], w_buf[k % OUT_SLOTS, :, columns], preferred_element_type=F32)
-            if k == 0:
-                total[:, columns] = product
-            elif k < nz - 1:
-                total[:, columns] = total[:, columns] + product
-            else:
-                out_ref[:, columns] = (x_ref[:, columns].astype(F32) + (total[:, columns] + product)).astype(BF16)
-            return carry
-
-        lax.fori_loop(low, high, tile, 0)
-        if high == tiles and k + OUT_SLOTS < nz:
-            fetch(k + OUT_SLOTS).start()
+                side_arrival(mirror[-sources[k]], s).wait_recv()
+            chip = z + way * sources[k]
+            for c in range(2):
+                for s in range(share):
+                    column = i * depth + (c * share + s) * head
+                    attended[:, column:column + head] = gathered[device(chip, c), s].astype(BF16)
+            fetch(k).wait()
+
+    def multiply(ks, n):
+        columns = pl.ds(n * OUT_TILE, OUT_TILE)
+        product = None
+        for i, k in enumerate(ks):
+            term = jnp.dot(attended[:, i * depth:(i + 1) * depth], w_buf[k % OUT_SLOTS, :, columns], preferred_element_type=F32)
+            product = term if product is None else product + term
+        if 0 in ks:
+            total[:, columns] = product
+        elif nz - 1 not in ks:
+            total[:, columns] = total[:, columns] + product
+        else:
+            out_ref[:, columns] = (x_ref[:, columns].astype(F32) + (total[:, columns] + product)).astype(BF16)
+            save(n).start()
+
+    def release(ks):
+        for k in ks:
+            if k + OUT_SLOTS < nz:
+                fetch(k + OUT_SLOTS).start()
 
     pending = [0]
     for hop in range(far):
-        work = [(k, n) for k in pending for n in range(2)]
+        work = list(range(tiles))
         for s in range(share):
             far_arrival(hop, s).wait_recv()
             if hop < far - 1:
@@ -366,15 +415,19 @@
                     back_copy(hop + 1, s).start()
                 side_copy(mirror[hop + 1], s).start()
             count = -(-len(work) // (share - s))
-            for k, n in work[:count]:
+            for n in work[:count]:
                 if n == 0:
-                    prepare(k)
-                multiply(k, n * tiles // 2, (n + 1) * tiles // 2)
+                    prepare(pending)
+                multiply(pending, n)
             work = work[count:]
-        pending = [mirror[-(hop + 1)]] + ([mirror[hop + 1]] if hop < far - 1 else [])
-    for k in pending:
-        prepare(k)
-        multiply(k, 0, tiles)
+        release(pending)
+        pending = sorted(set([mirror[-(hop + 1)], mirror[hop + 1]]))
+    fetch_x.wait()
+    prepare(pending)
+    for n in range(tiles):
+        multiply(pending, n)
+    for n in range(tiles):
+        save(n).wait()
 
     swap_stat.wait_send()
     for swap in swaps:
@@ -391,31 +444,38 @@
 
 
 def combine(num, stat, hidden, w_o, group):
-    heads, num_rows, head = num.shape
+    num_rows, width = hidden.shape
+    heads = num.shape[1] // ROW_BLOCK
+    head = num.shape[2]
     nz = group // 2
     share = heads // group
     far = nz // 2
-    width = w_o.shape[1]
     vmem = pl.BlockSpec(memory_space=pltpu.VMEM)
-    hbm = pl.BlockSpec(memory_space=pl.ANY)
+    hbm = pl.BlockSpec(memory_space=pltpu.HBM)
     dma = pltpu.SemaphoreType.DMA
     piece = (num_rows + 8, head)
     return pl.pallas_call(
         functools.partial(combine_kernel, nz),
         name='combine',
         out_shape=jax.ShapeDtypeStruct((num_rows, width), BF16),
-        in_specs=[vmem, vmem, vmem, hbm],
-        out_specs=vmem,
+        in_specs=[vmem, hbm, hbm, hbm],
+        out_specs=hbm,
         scratch_shapes=[
-            pltpu.VMEM((nz, share, num_rows, head), F32),
+            pltpu.VMEM((num_rows, width), BF16),
+            pltpu.VMEM((num_rows, width), BF16),
+            pltpu.VMEM((nz, num_rows // ROW_BLOCK, share * ROW_BLOCK, head), F32),
+            pltpu.VMEM((nz, num_rows // ROW_BLOCK, share * ROW_BLOCK, head), F32),
             pltpu.VMEM((2 * heads, num_rows), F32),
             pltpu.VMEM((nz, share) + piece, F32),
             pltpu.VMEM((far, share) + piece, F32),
             pltpu.VMEM((far - 1, share) + piece, F32),
             pltpu.VMEM((group, share, num_rows, head), F32),
             pltpu.VMEM((num_rows, width), F32),
-            pltpu.VMEM((num_rows, 2 * share * head), BF16),
+            pltpu.VMEM((num_rows, 4 * share * head), BF16),
             pltpu.VMEM((OUT_SLOTS, 2 * share * head, width), BF16),
+            dma((1,)),
+            dma((width // OUT_TILE,)),
+            dma((nz,)),
             dma((OUT_SLOTS,)),
             dma((2,)),
             dma((nz,)),
@@ -432,7 +492,7 @@
             dma((nz, share)),
         ],
         compiler_params=pltpu.CompilerParams(collective_id=1, has_side_effects=True, vmem_limit_bytes=62 * MIB),
-    )(num, stat, hidden, w_o)
+    )(stat, num, hidden, w_o)
 
 
 def solution(mesh):

time: 126 us -> 93 us (0.74)
  Pallas kernels: 114 us -> 89.1 us
  local copies, waits for them, and re-layouts: 9.89 us -> 2.69 us
  other arithmetic: 1.64 us -> 0 us
    pallas_call x1, Pallas kernels: 34.5 us -> 16.4 us  [attend(): pl.pallas_call(attend_kernel, name='attend', out_shape=(jax.ShapeDtypeStr...]
    pallas_call x1, Pallas kernels: 60 us -> 48.6 us  [combine(): pl.pallas_call(functools.partial(combine_kernel, nz), name='combine', out...]
    unnamed x17 -> x1, local copies, waits for them, and re-layouts: 9.17 us -> 2.69 us
    pallas_call x1, Pallas kernels: 19.5 us -> 24.1 us  [project(): pl.pallas_call(project_kernel, name='project', out_shape=(jax.ShapeDtypeS...]
where the time goes in v2:
time: 93 us; the launch traced here: 92.4 us
  Pallas kernels  89.1 us (96%)
  local copies, waits for them, and re-layouts  2.69 us (3%)
    pallas_call x1, Pallas kernels, combine(): pl.pallas_call(functools.partial(combine_kernel, nz), name='combine', out...  48.6 us
    pallas_call x1, Pallas kernels, project(): pl.pallas_call(project_kernel, name='project', out_shape=(jax.ShapeDtypeS...  24.1 us
    pallas_call x1, Pallas kernels, attend(): pl.pallas_call(attend_kernel, name='attend', out_shape=(jax.ShapeDtypeStr...  16.4 us
    unnamed x1, local copies, waits for them, and re-layouts  2.69 us

profile of v2, /device:TPU:21, one launch (start us, length us, event | category | flops | bytes accessed | tf_op | source)
XLA Modules:
  0.0 92.4 jit_solution(14134203863356778584)
XLA Ops:
  0.6 24.1 %project.1 = (f32[16,384,128]{2,1,0:T(8,128)}, f32[128,128]{1,0:T(8,128)}, f32[128,128]{1,0:T(8,128)}) custom-call(f32[1,128]{1,0:T(1,128)} %constant.2.clone.freq_ref, s32[1,128]{1,0:T(1,128)} %bitcast.1, bf16[6144]{0:T(1024)(128)(2,1)} %w_norm_ref.1, bf16[128,6144]{1,0:T(8,128)(2,1)} %x_hbm.3, bf16[6144,6144]{1,0:T(8,128)(2,1)} %w_q_ref.1, ...), custom_call_target="tpu_custom_call" | custom-call | tf_op jit(solution)/shard_map/project/pallas_call | solution.py:137
  24.7 16.4 %attend.1 = (bf16[128,128,128]{2,1,0:T(8,128)(2,1)}, bf16[128,128,128]{2,1,0:T(8,128)(2,1)}, f32[16,384,128]{2,1,0:T(8,128)}, f32[96,128]{1,0:T(8,128)}) custom-call(s32[128]{0:T(128)} %len_ref.1, f32[16,384,128]{2,1,0:T(8,128)} %get-tuple-element.10.q_ref, f32[128,128]{1,0:T(8,128)} %get-tuple-element.11.k_new_ref, f32[128,128]{1,0:T(8,128)} %get-tuple-element.12.v_new_ref, ...), custom_call_target="tpu_custom_call" | custom-call | tf_op jit(solution)/shard_map/attend/pallas_call | solution.py:205
  41.1 48.6 %combine.1 = bf16[128,6144]{1,0:T(8,128)(2,1)} custom-call(f32[96,128]{1,0:T(8,128)} %get-tuple-element.13.stat_ref, f32[16,384,128]{2,1,0:T(8,128)} %get-tuple-element.14.num_ref, bf16[128,6144]{1,0:T(8,128)(2,1)} %x_hbm.3, bf16[6144,6144]{1,0:T(8,128)(2,1)} %w_o_ref.1), custom_call_target="tpu_custom_call" | custom-call | tf_op jit(solution)/shard_map/combine/pallas_call | solution.py:457
  89.7 2.7 %copy.14 = bf16[128,6144]{1,0:T(8,128)(2,1)} copy(bf16[128,6144]{1,0:T(8,128)(2,1)} %combine.1) | data formatting | bytes 3145728

commit v3 on v2

--- a/solution.py
+++ b/solution.py
@@ -17,9 +17,8 @@
 MESH = pl.DeviceIdType.MESH
 TURN = (6.28125, 0.0019340515136718750, float(2 * np.pi - 6.28125 - 0.0019340515136718750))
 ROW_BLOCK = 8
-PROJ_SLOTS = 4
-OUT_SLOTS = 4
-OUT_TILE = 1536
+OUT_SLOTS = 12
+OUT_TILE = 3072
 
 
 def remote(src, dst, send_sem, recv_sem, device):
@@ -45,9 +44,8 @@
     first_head = core * half
 
     def fetch(block):
-        slot = (block + 1) % PROJ_SLOTS
         columns = pl.ds(pl.multiple_of((first_head + 2 * block) * head, pair), pair)
-        return pltpu.make_async_copy(w_q_ref.at[:, columns], w_buf.at[slot], w_sem.at[slot])
+        return pltpu.make_async_copy(w_q_ref.at[:, columns], w_buf.at[block + 1], w_sem.at[block])
 
     fetch_k = pltpu.make_async_copy(w_k_ref, w_buf.at[0, :, pl.ds(0, head)], kv_sem.at[0])
     fetch_v = pltpu.make_async_copy(w_v_ref, w_buf.at[0, :, pl.ds(head, head)], kv_sem.at[1])
@@ -55,7 +53,7 @@
     fetch_x.start()
     fetch_k.start()
     fetch_v.start()
-    for block in range(PROJ_SLOTS - 1):
+    for block in range(num_blocks):
         fetch(block).start()
 
     gain = 1.0 + w_norm_ref[...].astype(F32)
@@ -85,7 +83,6 @@
     both = jnp.dot(x_norm[...], w_buf[0], preferred_element_type=F32)
     k_ref[...] = rotate(both[:, :head]).astype(BF16).astype(F32)
     v_ref[...] = both[:, head:].astype(BF16).astype(F32)
-    fetch(PROJ_SLOTS - 1).start()
     enter([partner])
 
     def heads_of(c, block):
@@ -100,12 +97,7 @@
 
     def step(block, carry):
         fetch(block).wait()
-        product = jnp.dot(x_norm[...], w_buf[(block + 1) % PROJ_SLOTS], preferred_element_type=F32)
-
-        @pl.when(block + PROJ_SLOTS < num_blocks)
-        def _():
-            fetch(block + PROJ_SLOTS).start()
-
+        product = jnp.dot(x_norm[...], w_buf[block + 1], preferred_element_type=F32)
         for i in range(2):
             q = (rotate(product[:, i * head:(i + 1) * head]) * head ** -0.5).astype(BF16).astype(F32)
             q_buf[block, :, i * ROW_BLOCK:(i + 1) * ROW_BLOCK, :] = q.reshape(num_rows // ROW_BLOCK, ROW_BLOCK, head)
@@ -143,10 +135,10 @@
         scratch_shapes=[
             pltpu.VMEM((num_rows, width), BF16),
             pltpu.VMEM((num_rows, width), BF16),
-            pltpu.VMEM((PROJ_SLOTS, width, 2 * head), BF16),
+            pltpu.VMEM((blocks + 1, width, 2 * head), BF16),
             pltpu.VMEM((blocks, num_rows // ROW_BLOCK, 2 * ROW_BLOCK, head), F32),
             pltpu.SemaphoreType.DMA((1,)),
-            pltpu.SemaphoreType.DMA((PROJ_SLOTS,)),
+            pltpu.SemaphoreType.DMA((blocks,)),
             pltpu.SemaphoreType.DMA((2,)),
             pltpu.SemaphoreType.DMA((blocks,)),
             pltpu.SemaphoreType.DMA((blocks,)),
@@ -156,65 +148,101 @@
     )(inv_freq, cache_len.reshape(1, -1), w_norm, hidden, w_q, w_k, w_v)
 
 
-def attend_kernel(len_ref, q_ref, k_new_ref, v_new_ref, k_ref, v_ref, k_out, v_out, num_ref, stat_ref, scores_ref):
-    rows, slots, head = k_ref.shape
+def attend_kernel(len_ref, k_new_ref, v_new_ref, q_hbm, k_hbm, v_hbm, k_out_hbm, v_out_hbm, num_hbm, stat_ref, q_ref, k_ref, v_ref, num_ref, scores_ref, in_sem, out_sem):
+    num_rows, slots, head = k_ref.shape
+    rows = ROW_BLOCK
+    steps = num_rows // rows
     heads = stat_ref.shape[0] // 2
     base = lax.axis_index('sp') * slots
-    first = pl.program_id(0) * rows
     group_iota = lax.broadcasted_iota(jnp.int32, (16, head), 0)
     lane_iota = lax.broadcasted_iota(jnp.int32, (heads, slots), 1)
-    places = [len_ref[first + r] - base for r in range(rows)]
-    for new, old, out in ((k_new_ref, k_ref, k_out), (v_new_ref, v_ref, v_out)):
-        out[...] = old[...]
+
+    def loads(step):
+        block = pl.ds(step * rows, rows)
+        return [pltpu.make_async_copy(src, dst, in_sem.at[i, step]) for i, (src, dst) in enumerate(((k_hbm.at[block], k_ref.at[block]), (v_hbm.at[block], v_ref.at[block]), (q_hbm.at[step], q_ref.at[step])))]
+
+    def stores(step):
+        block = pl.ds(step * rows, rows)
+        return [pltpu.make_async_copy(src, dst, out_sem.at[i, step]) for i, (src, dst) in enumerate(((k_ref.at[block], k_out_hbm.at[block]), (v_ref.at[block], v_out_hbm.at[block]), (num_ref.at[step], num_hbm.at[step])))]
+
+    def start(step, carry):
+        for copy in loads(step):
+            copy.start()
+        return carry
+
+    def attend_rows(step, carry):
+        first = step * rows
+        for copy in loads(step):
+            copy.wait()
+        places = [len_ref[first + r] - base for r in range(rows)]
+        for new, cache in ((k_new_ref, k_ref), (v_new_ref, v_ref)):
+            fresh = new[pl.ds(pl.multiple_of(first, rows), rows), :]
+            for r, p in enumerate(places):
+                group = pl.multiple_of(jnp.clip(p, 0, slots - 1) // 16 * 16, 16)
+                tile = cache[first + r, pl.ds(group, 16), :].astype(F32)
+                cache[first + r, pl.ds(group, 16), :] = jnp.where(group_iota == p - group, fresh[r:r + 1, :], tile).astype(BF16)
+        queries = q_ref.at[step]
+        for r in range(rows):
+            q = queries[pl.ds(r, heads, stride=rows), :].astype(BF16)
+            scores_ref[r] = lax.dot_general(q, k_ref[first + r], (((1,), (1,)), ((), ())), preferred_element_type=F32)
+        maxima, totals, factors = [], [], []
         for r, p in enumerate(places):
-            group = pl.multiple_of(jnp.clip(p, 0, slots - 1) // 16 * 16, 16)
-            tile = old[r, pl.ds(group, 16), :].astype(F32)
-            out[r, pl.ds(group, 16), :] = jnp.where(group_iota == p - group, new[r:r + 1, :], tile).astype(BF16)
-    for r in range(rows):
-        q = q_ref[pl.ds(r, heads, stride=rows), :].astype(BF16)
-        scores_ref[r] = lax.dot_general(q, k_out[r], (((1,), (1,)), ((), ())), preferred_element_type=F32)
-    maxima, totals, factors = [], [], []
-    for r, p in enumerate(places):
-        valid = lane_iota <= p
-        scores = jnp.where(valid, scores_ref[r], FLOOR)
-        row_max = jnp.max(scores, axis=1, keepdims=True)
-        weights = jnp.where(valid, jnp.exp(scores - row_max), 0.0)
-        maxima.append(row_max)
-        totals.append(jnp.sum(weights, axis=1, keepdims=True))
-        factors.append(weights.astype(BF16))
-    for r in range(rows):
-        num_ref[pl.ds(r, heads, stride=rows), :] = jnp.dot(factors[r], v_out[r], preferred_element_type=F32)
-    stat_m = stat_ref[0:heads, :]
-    stat_l = stat_ref[heads:2 * heads, :]
-    for r in range(rows):
-        here = lane_iota == first + r
-        stat_m = jnp.where(here, maxima[r], stat_m)
-        stat_l = jnp.where(here, totals[r], stat_l)
-    stat_ref[0:heads, :] = stat_m
-    stat_ref[heads:2 * heads, :] = stat_l
+            valid = lane_iota <= p
+            scores = jnp.where(valid, scores_ref[r], FLOOR)
+            row_max = jnp.max(scores, axis=1, keepdims=True)
+            weights = jnp.where(valid, jnp.exp(scores - row_max), 0.0)
+            maxima.append(row_max)
+            totals.append(jnp.sum(weights, axis=1, keepdims=True))
+            factors.append(weights.astype(BF16))
+        partial = num_ref.at[step]
+        for r in range(rows):
+            partial[pl.ds(r, heads, stride=rows), :] = jnp.dot(factors[r], v_ref[first + r], preferred_element_type=F32)
+        stat_m = stat_ref[0:heads, :]
+        stat_l = stat_ref[heads:2 * heads, :]
+        for r in range(rows):
+            here = lane_iota == first + r
+            stat_m = jnp.where(here, maxima[r], stat_m)
+            stat_l = jnp.where(here, totals[r], stat_l)
+        stat_ref[0:heads, :] = stat_m
+        stat_ref[heads:2 * heads, :] = stat_l
+        for copy in stores(step):
+            copy.start()
+        return carry
+
+    def finish(step, carry):
+        for copy in stores(step):
+            copy.wait()
+        return carry
+
+    lax.fori_loop(0, steps, start, 0)
+    lax.fori_loop(0, steps, attend_rows, 0)
+    lax.fori_loop(0, steps, finish, 0)
 
 
 def attend(q, k_new, v_new, k_block, v_block, cache_len):
     num_rows, slots, head = k_block.shape
-    rows = ROW_BLOCK
-    heads = q.shape[1] // rows
-    by_head = pl.BlockSpec((None, heads * rows, head), lambda i, *_: (i, 0, 0))
-    by_row = pl.BlockSpec((rows, head), lambda i, *_: (i, 0))
-    cache = pl.BlockSpec((rows, slots, head), lambda i, *_: (i, 0, 0))
-    stats = pl.BlockSpec((2 * heads, num_rows), lambda i, *_: (0, 0))
+    steps = num_rows // ROW_BLOCK
+    heads = q.shape[1] // ROW_BLOCK
+    smem = pl.BlockSpec(memory_space=pltpu.SMEM)
+    vmem = pl.BlockSpec(memory_space=pltpu.VMEM)
+    hbm = pl.BlockSpec(memory_space=pltpu.HBM)
     return pl.pallas_call(
         attend_kernel,
         name='attend',
         out_shape=(jax.ShapeDtypeStruct(k_block.shape, BF16), jax.ShapeDtypeStruct(v_block.shape, BF16), jax.ShapeDtypeStruct(q.shape, F32), jax.ShapeDtypeStruct((2 * heads, num_rows), F32)),
-        grid_spec=pltpu.PrefetchScalarGridSpec(
-            num_scalar_prefetch=1,
-            grid=(num_rows // rows,),
-            in_specs=[by_head, by_row, by_row, cache, cache],
-            out_specs=(cache, cache, by_head, stats),
-            scratch_shapes=[pltpu.VMEM((rows, heads, slots), F32)],
-        ),
-        compiler_params=pltpu.CompilerParams(dimension_semantics=('arbitrary',), vmem_limit_bytes=60 * MIB),
-    )(cache_len, q, k_new, v_new, k_block, v_block)
+        in_specs=[smem, vmem, vmem, hbm, hbm, hbm],
+        out_specs=(hbm, hbm, hbm, vmem),
+        scratch_shapes=[
+            pltpu.VMEM(q.shape, F32),
+            pltpu.VMEM(k_block.shape, BF16),
+            pltpu.VMEM(v_block.shape, BF16),
+            pltpu.VMEM(q.shape, F32),
+            pltpu.VMEM((ROW_BLOCK, heads, slots), F32),
+            pltpu.SemaphoreType.DMA((3, steps)),
+            pltpu.SemaphoreType.DMA((3, steps)),
+        ],
+        compiler_params=pltpu.CompilerParams(vmem_limit_bytes=60 * MIB),
+    )(cache_len, k_new, v_new, q, k_block, v_block)
 
 
 def combine_kernel(nz, stat_ref, num_ref, x_hbm, w_o_ref, out_hbm, x_ref, out_ref, own_num, near_num, near_stat, part, from_long, from_short, gathered, total, attended, w_buf, x_sem, out_sem, own_sem, w_sem, stat_sem, near_send, near_recv, long_send, long_recv, short_send, short_recv, far_send, far_recv, back_send, back_recv, side_send, side_recv):
@@ -228,7 +256,6 @@
     head = num_ref.shape[2]
     share = heads // (2 * nz)
     far = nz // 2
-    depth = 2 * share * head
 
     def device(chip, c):
         return (chip + 2 * nz) % nz * 2 + c
@@ -244,9 +271,20 @@
         sources += [-hop, hop]
     sources.append(-far)
 
-    def fetch(k):
-        chip = device(z + way * sources[k], 0) // 2
-        return pltpu.make_async_copy(w_o_ref.at[pl.ds(pl.multiple_of(chip * depth, depth), depth), :], w_buf.at[k % OUT_SLOTS], w_sem.at[k % OUT_SLOTS])
+    units = [(0, s) for s in range(share)]
+    for hop in range(1, far):
+        units += [(sources.index(step), s) for s in range(share) for step in (-hop, hop)]
+    units += [(nz - 1, s) for s in range(share)]
+
+    def fetch(u):
+        k, s = units[u]
+        chip = z + way * sources[k]
+        rows = [pl.ds(pl.multiple_of((device(chip, c) * share + s) * head, head), head) for c in range(2)]
+        return [pltpu.make_async_copy(w_o_ref.at[rows[c], :], w_buf.at[u % OUT_SLOTS, c * head:(c + 1) * head, :], w_sem.at[u % OUT_SLOTS, c]) for c in range(2)]
+
+    def start_fetch(u):
+        for copy in fetch(u):
+            copy.start()
 
     def own_heads(i, c):
         way_c = way * (1 - 2 * c)
@@ -268,7 +306,7 @@
     fetch_x = pltpu.make_async_copy(x_hbm, x_ref, x_sem.at[0])
     fetch_x.start()
     for k in range(OUT_SLOTS):
-        fetch(k).start()
+        start_fetch(k)
 
     def column(row):
         return jnp.broadcast_to(row, (num_rows, num_rows)).T
@@ -371,39 +409,44 @@
         columns = pl.ds(pl.multiple_of(n * OUT_TILE, OUT_TILE), OUT_TILE)
         return pltpu.make_async_copy(out_ref.at[:, columns], out_hbm.at[:, columns], out_sem.at[n])
 
-    def prepare(ks):
-        for i, k in enumerate(ks):
-            for s in range(share):
-                side_arrival(mirror[-sources[k]], s).wait_recv()
+    def multiply(us):
+        for i, u in enumerate(us):
+            k, s = units[u]
+            side_arrival(mirror[-sources[k]], s).wait_recv()
             chip = z + way * sources[k]
             for c in range(2):
-                for s in range(share):
-                    column = i * depth + (c * share + s) * head
-                    attended[:, column:column + head] = gathered[device(chip, c), s].astype(BF16)
-            fetch(k).wait()
-
-    def multiply(ks, n):
-        columns = pl.ds(n * OUT_TILE, OUT_TILE)
-        product = None
-        for i, k in enumerate(ks):
-            term = jnp.dot(attended[:, i * depth:(i + 1) * depth], w_buf[k % OUT_SLOTS, :, columns], preferred_element_type=F32)
-            product = term if product is None else product + term
-        if 0 in ks:
-            total[:, columns] = product
-        elif nz - 1 not in ks:
-            total[:, columns] = total[:, columns] + product
-        else:
-            out_ref[:, columns] = (x_ref[:, columns].astype(F32) + (total[:, columns] + product)).astype(BF16)
-            save(n).start()
-
-    def release(ks):
-        for k in ks:
-            if k + OUT_SLOTS < nz:
-                fetch(k + OUT_SLOTS).start()
-
-    pending = [0]
+                attended[i, :, c * head:(c + 1) * head] = gathered[device(chip, c), s].astype(BF16)
+            for copy in fetch(u):
+                copy.wait()
+
+        def tile(n, carry):
+            columns = pl.ds(pl.multiple_of(n * OUT_TILE, OUT_TILE), OUT_TILE)
+            product = None
+            for i, u in enumerate(us):
+                term = jnp.dot(attended[i], w_buf[u % OUT_SLOTS, :, columns], preferred_element_type=F32)
+                product = term if product is None else product + term
+            before = x_ref[:, columns].astype(F32) if 0 in us else total[:, columns]
+            if len(units) - 1 in us:
+                out_ref[:, columns] = (before + product).astype(BF16)
+                save(n).start()
+            else:
+                total[:, columns] = before + product
+            return carry
+
+        lax.fori_loop(0, tiles, tile, 0)
+        for u in us:
+            if u + OUT_SLOTS < len(units):
+                start_fetch(u + OUT_SLOTS)
+
+    chunks = [[s] for s in range(share)]
+    while sum(map(len, chunks)) < len(units) - share:
+        u = sum(map(len, chunks))
+        chunks.append([u, u + 1])
+    chunks += [[len(units) - share + s] for s in range(share)]
+    fetch_x.wait()
+    multiply(chunks.pop(0))
+    multiply(chunks.pop(0))
     for hop in range(far):
-        work = list(range(tiles))
         for s in range(share):
             far_arrival(hop, s).wait_recv()
             if hop < far - 1:
@@ -414,18 +457,9 @@
                 if hop < far - 2:
                     back_copy(hop + 1, s).start()
                 side_copy(mirror[hop + 1], s).start()
-            count = -(-len(work) // (share - s))
-            for n in work[:count]:
-                if n == 0:
-                    prepare(pending)
-                multiply(pending, n)
-            work = work[count:]
-        release(pending)
-        pending = sorted(set([mirror[-(hop + 1)], mirror[hop + 1]]))
-    fetch_x.wait()
-    prepare(pending)
-    for n in range(tiles):
-        multiply(pending, n)
+            multiply(chunks.pop(0))
+    for chunk in chunks:
+        multiply(chunk)
     for n in range(tiles):
         save(n).wait()
 
@@ -471,12 +505,12 @@
             pltpu.VMEM((far - 1, share) + piece, F32),
             pltpu.VMEM((group, share, num_rows, head), F32),
             pltpu.VMEM((num_rows, width), F32),
-            pltpu.VMEM((num_rows, 4 * share * head), BF16),
-            pltpu.VMEM((OUT_SLOTS, 2 * share * head, width), BF16),
+            pltpu.VMEM((2, num_rows, 2 * head), BF16),
+            pltpu.VMEM((OUT_SLOTS, 2 * head, width), BF16),
             dma((1,)),
             dma((width // OUT_TILE,)),
             dma((nz,)),
-            dma((OUT_SLOTS,)),
+            dma((OUT_SLOTS, 2)),
             dma((2,)),
             dma((nz,)),
             dma((nz,)),

time: 93 us -> 94.2 us (1.013)
  Pallas kernels: 89.1 us -> 90.6 us
    pallas_call x1, Pallas kernels: 24.1 us -> 30.3 us  [project(): pl.pallas_call(project_kernel, name='project', out_shape=(jax.ShapeDtypeS...]
    pallas_call x1, Pallas kernels: 16.4 us -> 13.6 us  [attend(): pl.pallas_call(attend_kernel, name='attend', out_shape=(jax.ShapeDtypeStr...]
    pallas_call x1, Pallas kernels: 48.6 us -> 46.8 us  [combine(): pl.pallas_call(functools.partial(combine_kernel, nz), name='combine', out...]
where the time goes in v3:
time: 94.2 us; the launch traced here: 93.9 us
  Pallas kernels  90.6 us (96%)
  local copies, waits for them, and re-layouts  2.69 us (3%)
    pallas_call x1, Pallas kernels, combine(): pl.pallas_call(functools.partial(combine_kernel, nz), name='combine', out...  46.8 us
    pallas_call x1, Pallas kernels, project(): pl.pallas_call(project_kernel, name='project', out_shape=(jax.ShapeDtypeS...  30.3 us
    pallas_call x1, Pallas kernels, attend(): pl.pallas_call(attend_kernel, name='attend', out_shape=(jax.ShapeDtypeStr...  13.6 us
    unnamed x1, local copies, waits for them, and re-layouts  2.69 us

profile of v3, /device:TPU:21, one launch (start us, length us, event | category | flops | bytes accessed | tf_op | source)
XLA Modules:
  0.0 93.9 jit_solution(11504581207240052007)
XLA Ops:
  0.6 30.3 %project.1 = (f32[16,384,128]{2,1,0:T(8,128)}, f32[128,128]{1,0:T(8,128)}, f32[128,128]{1,0:T(8,128)}) custom-call(f32[1,128]{1,0:T(1,128)} %constant.2.clone.freq_ref, s32[1,128]{1,0:T(1,128)} %bitcast.1, bf16[6144]{0:T(1024)(128)(2,1)} %w_norm_ref.1, bf16[128,6144]{1,0:T(8,128)(2,1)} %x_hbm.3, bf16[6144,6144]{1,0:T(8,128)(2,1)} %w_q_ref.1, ...), custom_call_target="tpu_custom_call" | custom-call | tf_op jit(solution)/shard_map/project/pallas_call | solution.py:129
  30.9 13.6 %attend.1 = (bf16[128,128,128]{2,1,0:T(8,128)(2,1)}, bf16[128,128,128]{2,1,0:T(8,128)(2,1)}, f32[16,384,128]{2,1,0:T(8,128)}, f32[96,128]{1,0:T(8,128)}) custom-call(s32[128]{0:T(128)} %len_ref.1, f32[128,128]{1,0:T(8,128)} %get-tuple-element.10.k_new_ref, f32[128,128]{1,0:T(8,128)} %get-tuple-element.11.v_new_ref, f32[16,384,128]{2,1,0:T(8,128)} %get-tuple-element.12.q_hbm, ...), custom_call_target="tpu_custom_call" | custom-call | tf_op jit(solution)/shard_map/attend/pallas_call | solution.py:229
  44.5 46.8 %combine.1 = bf16[128,6144]{1,0:T(8,128)(2,1)} custom-call(f32[96,128]{1,0:T(8,128)} %get-tuple-element.13.stat_ref, f32[16,384,128]{2,1,0:T(8,128)} %get-tuple-element.14.num_ref, bf16[128,6144]{1,0:T(8,128)(2,1)} %x_hbm.3, bf16[6144,6144]{1,0:T(8,128)(2,1)} %w_o_ref.1), custom_call_target="tpu_custom_call" | custom-call | tf_op jit(solution)/shard_map/combine/pallas_call | solution.py:491
  91.2 2.7 %copy.14 = bf16[128,6144]{1,0:T(8,128)(2,1)} copy(bf16[128,6144]{1,0:T(8,128)(2,1)} %combine.1) | data formatting | bytes 3145728

commit v4 on v3

--- a/solution.py
+++ b/solution.py
@@ -18,6 +18,8 @@
 TURN = (6.28125, 0.0019340515136718750, float(2 * np.pi - 6.28125 - 0.0019340515136718750))
 ROW_BLOCK = 8
 OUT_SLOTS = 12
+PROJ_WINDOW = 4
+ATTEND_WINDOW = 4
 OUT_TILE = 3072
 
 
@@ -53,8 +55,7 @@
     fetch_x.start()
     fetch_k.start()
     fetch_v.start()
-    for block in range(num_blocks):
-        fetch(block).start()
+    fetch(0).start()
 
     gain = 1.0 + w_norm_ref[...].astype(F32)
     angles = jnp.broadcast_to(len_ref[...].astype(F32), (num_rows, num_rows)).T * freq_ref[...]
@@ -64,6 +65,8 @@
     cos_t = jnp.cos(angles)
     sin_t = jnp.where(lax.broadcasted_iota(jnp.int32, angles.shape, 1) < head // 2, -1.0, 1.0) * jnp.sin(angles)
     fetch_x.wait()
+    for block in range(1, PROJ_WINDOW):
+        fetch(block).start()
 
     def normalise(step, carry):
         rows = pl.ds(pl.multiple_of(step * 16, 16), 16)
@@ -96,6 +99,10 @@
         return remote(q_buf.at[block], heads_of(core, block), send_sem.at[block], recv_sem.at[block], partner)
 
     def step(block, carry):
+        @pl.when(block + PROJ_WINDOW < num_blocks)
+        def _():
+            fetch(block + PROJ_WINDOW).start()
+
         fetch(block).wait()
         product = jnp.dot(x_norm[...], w_buf[block + 1], preferred_element_type=F32)
         for i in range(2):
@@ -172,6 +179,11 @@
 
     def attend_rows(step, carry):
         first = step * rows
+
+        @pl.when(step + ATTEND_WINDOW < steps)
+        def _():
+            start(step + ATTEND_WINDOW, 0)
+
         for copy in loads(step):
             copy.wait()
         places = [len_ref[first + r] - base for r in range(rows)]
@@ -214,7 +226,7 @@
             copy.wait()
         return carry
 
-    lax.fori_loop(0, steps, start, 0)
+    lax.fori_loop(0, ATTEND_WINDOW, start, 0)
     lax.fori_loop(0, steps, attend_rows, 0)
     lax.fori_loop(0, steps, finish, 0)
 
@@ -304,9 +316,12 @@
         swap.start()
         swaps.append(swap)
     fetch_x = pltpu.make_async_copy(x_hbm, x_ref, x_sem.at[0])
-    fetch_x.start()
-    for k in range(OUT_SLOTS):
-        start_fetch(k)
+    ahead_of_use = list(range(OUT_SLOTS))
+
+    def fetch_some(count):
+        for _ in range(count):
+            if ahead_of_use:
+                start_fetch(ahead_of_use.pop(0))
 
     def column(row):
         return jnp.broadcast_to(row, (num_rows, num_rows)).T
@@ -355,11 +370,14 @@
         if hop == 0:
             for s in range(share):
                 short_copy(0, s).start()
+            fetch_x.start()
+            fetch_some(2)
             continue
         for s in range(share):
             long_copy(hop - 1, s).wait_recv()
             store(part.at[2 * hop, s], merge(load(part.at[2 * hop, s]), load(from_long.at[hop - 1, s])))
             long_copy(hop, s).start()
+            fetch_some(2)
             if hop < far - 1:
                 short_copy(hop - 1, s).wait_recv()
                 store(part.at[2 * hop + 1, s], merge(load(part.at[2 * hop + 1, s]), load(from_short.at[hop - 1, s])))
@@ -393,6 +411,7 @@
     mirror[far] = mirror[-far]
 
     last = far - 1
+    fetch_some(OUT_SLOTS)
     for s in range(share):
         short_copy(last - 1, s).wait_recv()
         triple = merge(load(part.at[2 * far - 1, s]), load(from_short.at[last - 1, s]))

time: 94.2 us -> 85.9 us (0.912)
  Pallas kernels: 90.6 us -> 82.3 us
    pallas_call x1, Pallas kernels: 30.3 us -> 22.1 us  [project(): pl.pallas_call(project_kernel, name='project', out_shape=(jax.ShapeDtypeS...]
where the time goes in v4:
time: 85.9 us; the launch traced here: 85.7 us
  Pallas kernels  82.3 us (96%)
  local copies, waits for them, and re-layouts  2.69 us (3%)
    pallas_call x1, Pallas kernels, combine(): pl.pallas_call(functools.partial(combine_kernel, nz), name='combine', out...  46.6 us
    pallas_call x1, Pallas kernels, project(): pl.pallas_call(project_kernel, name='project', out_shape=(jax.ShapeDtypeS...  22.1 us
    pallas_call x1, Pallas kernels, attend(): pl.pallas_call(attend_kernel, name='attend', out_shape=(jax.ShapeDtypeStr...  13.7 us
    unnamed x1, local copies, waits for them, and re-layouts  2.69 us

profile of v4, /device:TPU:21, one launch (start us, length us, event | category | flops | bytes accessed | tf_op | source)
XLA Modules:
  0.0 85.7 jit_solution(1646746194252387497)
XLA Ops:
  0.6 22.1 %project.1 = (f32[16,384,128]{2,1,0:T(8,128)}, f32[128,128]{1,0:T(8,128)}, f32[128,128]{1,0:T(8,128)}) custom-call(f32[1,128]{1,0:T(1,128)} %constant.2.clone.freq_ref, s32[1,128]{1,0:T(1,128)} %bitcast.1, bf16[6144]{0:T(1024)(128)(2,1)} %w_norm_ref.1, bf16[128,6144]{1,0:T(8,128)(2,1)} %x_hbm.3, bf16[6144,6144]{1,0:T(8,128)(2,1)} %w_q_ref.1, ...), custom_call_target="tpu_custom_call" | custom-call | tf_op jit(solution)/shard_map/project/pallas_call | solution.py:136
  22.7 13.7 %attend.1 = (bf16[128,128,128]{2,1,0:T(8,128)(2,1)}, bf16[128,128,128]{2,1,0:T(8,128)(2,1)}, f32[16,384,128]{2,1,0:T(8,128)}, f32[96,128]{1,0:T(8,128)}) custom-call(s32[128]{0:T(128)} %len_ref.1, f32[128,128]{1,0:T(8,128)} %get-tuple-element.10.k_new_ref, f32[128,128]{1,0:T(8,128)} %get-tuple-element.11.v_new_ref, f32[16,384,128]{2,1,0:T(8,128)} %get-tuple-element.12.q_hbm, ...), custom_call_target="tpu_custom_call" | custom-call | tf_op jit(solution)/shard_map/attend/pallas_call | solution.py:241
  36.4 46.6 %combine.1 = bf16[128,6144]{1,0:T(8,128)(2,1)} custom-call(f32[96,128]{1,0:T(8,128)} %get-tuple-element.13.stat_ref, f32[16,384,128]{2,1,0:T(8,128)} %get-tuple-element.14.num_ref, bf16[128,6144]{1,0:T(8,128)(2,1)} %x_hbm.3, bf16[6144,6144]{1,0:T(8,128)(2,1)} %w_o_ref.1), custom_call_target="tpu_custom_call" | custom-call | tf_op jit(solution)/shard_map/combine/pallas_call | solution.py:510
  83.0 2.7 %copy.14 = bf16[128,6144]{1,0:T(8,128)(2,1)} copy(bf16[128,6144]{1,0:T(8,128)(2,1)} %combine.1) | data formatting | bytes 3145728

commit v5 on v4

--- a/solution.py
+++ b/solution.py
@@ -19,7 +19,8 @@
 ROW_BLOCK = 8
 OUT_SLOTS = 12
 PROJ_WINDOW = 4
-ATTEND_WINDOW = 4
+ATTEND_WINDOW = 3
+ATTEND_BLOCKS = 2
 OUT_TILE = 3072
 
 
@@ -155,9 +156,10 @@
     )(inv_freq, cache_len.reshape(1, -1), w_norm, hidden, w_q, w_k, w_v)
 
 
-def attend_kernel(len_ref, k_new_ref, v_new_ref, q_hbm, k_hbm, v_hbm, k_out_hbm, v_out_hbm, num_hbm, stat_ref, q_ref, k_ref, v_ref, num_ref, scores_ref, in_sem, out_sem):
+def attend_kernel(len_ref, k_new_ref, v_new_ref, q_hbm, k_hbm, v_hbm, k_out_hbm, v_out_hbm, num_hbm, stat_ref, q_ref, k_ref, v_ref, num_ref, scores_ref, factors_ref, in_sem, out_sem):
     num_rows, slots, head = k_ref.shape
-    rows = ROW_BLOCK
+    blocks = ATTEND_BLOCKS
+    rows = ROW_BLOCK * blocks
     steps = num_rows // rows
     heads = stat_ref.shape[0] // 2
     base = lax.axis_index('sp') * slots
@@ -166,11 +168,14 @@
 
     def loads(step):
         block = pl.ds(step * rows, rows)
-        return [pltpu.make_async_copy(src, dst, in_sem.at[i, step]) for i, (src, dst) in enumerate(((k_hbm.at[block], k_ref.at[block]), (v_hbm.at[block], v_ref.at[block]), (q_hbm.at[step], q_ref.at[step])))]
+        part = pl.ds(step * blocks, blocks)
+        sem = in_sem.at[lax.rem(step, ATTEND_WINDOW + 1)]
+        return [pltpu.make_async_copy(src, dst, sem) for src, dst in ((k_hbm.at[block], k_ref.at[block]), (v_hbm.at[block], v_ref.at[block]), (q_hbm.at[part], q_ref.at[part]))]
 
     def stores(step):
         block = pl.ds(step * rows, rows)
-        return [pltpu.make_async_copy(src, dst, out_sem.at[i, step]) for i, (src, dst) in enumerate(((k_ref.at[block], k_out_hbm.at[block]), (v_ref.at[block], v_out_hbm.at[block]), (num_ref.at[step], num_hbm.at[step])))]
+        part = pl.ds(step * blocks, blocks)
+        return [pltpu.make_async_copy(src, dst, out_sem.at[0]) for src, dst in ((k_ref.at[block], k_out_hbm.at[block]), (v_ref.at[block], v_out_hbm.at[block]), (num_ref.at[part], num_hbm.at[part]))]
 
     def start(step, carry):
         for copy in loads(step):
@@ -193,30 +198,26 @@
                 group = pl.multiple_of(jnp.clip(p, 0, slots - 1) // 16 * 16, 16)
                 tile = cache[first + r, pl.ds(group, 16), :].astype(F32)
                 cache[first + r, pl.ds(group, 16), :] = jnp.where(group_iota == p - group, fresh[r:r + 1, :], tile).astype(BF16)
-        queries = q_ref.at[step]
         for r in range(rows):
-            q = queries[pl.ds(r, heads, stride=rows), :].astype(BF16)
+            queries = q_ref.at[step * blocks + r // ROW_BLOCK]
+            q = queries[pl.ds(r % ROW_BLOCK, heads, stride=ROW_BLOCK), :].astype(BF16)
             scores_ref[r] = lax.dot_general(q, k_ref[first + r], (((1,), (1,)), ((), ())), preferred_element_type=F32)
-        maxima, totals, factors = [], [], []
+        stat_m = stat_ref[0:heads, :]
+        stat_l = stat_ref[heads:2 * heads, :]
         for r, p in enumerate(places):
             valid = lane_iota <= p
             scores = jnp.where(valid, scores_ref[r], FLOOR)
             row_max = jnp.max(scores, axis=1, keepdims=True)
             weights = jnp.where(valid, jnp.exp(scores - row_max), 0.0)
-            maxima.append(row_max)
-            totals.append(jnp.sum(weights, axis=1, keepdims=True))
-            factors.append(weights.astype(BF16))
-        partial = num_ref.at[step]
-        for r in range(rows):
-            partial[pl.ds(r, heads, stride=rows), :] = jnp.dot(factors[r], v_ref[first + r], preferred_element_type=F32)
-        stat_m = stat_ref[0:heads, :]
-        stat_l = stat_ref[heads:2 * heads, :]
-        for r in range(rows):
             here = lane_iota == first + r
-            stat_m = jnp.where(here, maxima[r], stat_m)
-            stat_l = jnp.where(here, totals[r], stat_l)
+            stat_m = jnp.where(here, row_max, stat_m)
+            stat_l = jnp.where(here, jnp.sum(weights, axis=1, keepdims=True), stat_l)
+            factors_ref[r] = weights.astype(BF16)
         stat_ref[0:heads, :] = stat_m
         stat_ref[heads:2 * heads, :] = stat_l
+        for r in range(rows):
+            partial = num_ref.at[step * blocks + r // ROW_BLOCK]
+            partial[pl.ds(r % ROW_BLOCK, heads, stride=ROW_BLOCK), :] = jnp.dot(factors_ref[r], v_ref[first + r], preferred_element_type=F32)
         for copy in stores(step):
             copy.start()
         return carry
@@ -233,7 +234,6 @@
 
 def attend(q, k_new, v_new, k_block, v_block, cache_len):
     num_rows, slots, head = k_block.shape
-    steps = num_rows // ROW_BLOCK
     heads = q.shape[1] // ROW_BLOCK
     smem = pl.BlockSpec(memory_space=pltpu.SMEM)
     vmem = pl.BlockSpec(memory_space=pltpu.VMEM)
@@ -249,15 +249,16 @@
             pltpu.VMEM(k_block.shape, BF16),
             pltpu.VMEM(v_block.shape, BF16),
             pltpu.VMEM(q.shape, F32),
-            pltpu.VMEM((ROW_BLOCK, heads, slots), F32),
-            pltpu.SemaphoreType.DMA((3, steps)),
-            pltpu.SemaphoreType.DMA((3, steps)),
+            pltpu.VMEM((ATTEND_BLOCKS * ROW_BLOCK, heads, slots), F32),
+            pltpu.VMEM((ATTEND_BLOCKS * ROW_BLOCK, heads, slots), BF16),
+            pltpu.SemaphoreType.DMA((ATTEND_WINDOW + 1,)),
+            pltpu.SemaphoreType.DMA((1,)),
         ],
         compiler_params=pltpu.CompilerParams(vmem_limit_bytes=60 * MIB),
     )(cache_len, k_new, v_new, q, k_block, v_block)
 
 
-def combine_kernel(nz, stat_ref, num_ref, x_hbm, w_o_ref, out_hbm, x_ref, out_ref, own_num, near_num, near_stat, part, from_long, from_short, gathered, total, attended, w_buf, x_sem, out_sem, own_sem, w_sem, stat_sem, near_send, near_recv, long_send, long_recv, short_send, short_recv, far_send, far_recv, back_send, back_recv, side_send, side_recv):
+def combine_kernel(nz, stat_ref, num_ref, x_hbm, w_o_ref, out_hbm, x_ref, out_ref, own_num, sent_num, near_num, near_stat, part, from_long, from_short, gathered, total, attended, w_buf, x_sem, out_sem, own_sem, w_sem, stat_sem, near_send, near_recv, long_send, long_recv, short_send, short_recv, far_send, far_recv, back_send, back_recv, side_send, side_recv):
     me = lax.axis_index('sp')
     z = me // 2
     core = me % 2
@@ -304,17 +305,28 @@
         first = rows * device(z + way_c * targets[i], core + way * c)
         return num_ref.at[:, pl.ds(pl.multiple_of(first, rows), rows), :]
 
-    own_copies = [pltpu.make_async_copy(own_heads(i, 0), own_num.at[i], own_sem.at[i]) for i in range(nz)]
-    for copy in own_copies:
-        copy.start()
+    def stage(i):
+        return [pltpu.make_async_copy(own_heads(i, 1), sent_num.at[i], own_sem.at[1, i]), pltpu.make_async_copy(own_heads(i, 0), own_num.at[i], own_sem.at[0, i])]
+
+    stages = [stage(i) for i in range(nz)]
+    swap_stat = remote(stat_ref, near_stat, stat_sem.at[0], stat_sem.at[1], partner)
+    swaps = [remote(sent_num.at[i], near_num.at[i], near_send.at[i], near_recv.at[i], partner) for i in range(nz)]
+
+    def start_swaps(low, high):
+        for i in range(low, high):
+            stages[i][0].wait()
+            swaps[i].start()
+
+    for i in range(2):
+        for copy in stages[i]:
+            copy.start()
     enter([partner, ahead, behind])
-    swap_stat = remote(stat_ref, near_stat, stat_sem.at[0], stat_sem.at[1], partner)
     swap_stat.start()
-    swaps = []
-    for i in range(nz):
-        swap = remote(own_heads(i, 1), near_num.at[i], near_send.at[i], near_recv.at[i], partner)
-        swap.start()
-        swaps.append(swap)
+    start_swaps(0, 2)
+    for i in range(2, nz):
+        for copy in stages[i]:
+            copy.start()
+    start_swaps(2, 4)
     fetch_x = pltpu.make_async_copy(x_hbm, x_ref, x_sem.at[0])
     ahead_of_use = list(range(OUT_SLOTS))
 
@@ -343,15 +355,18 @@
         ref[0:num_rows, :] = x
         ref[num_rows:num_rows + 8, :] = jnp.where(sub_iota == 0, m, l)
 
-    def own(i):
-        own_copies[i].wait()
+    def own(i, send=None):
+        stages[i][1].wait()
         swaps[i].wait_recv()
         first = share * device(z + way * targets[i], core)
         for s in range(share):
             h = first + s
-            mine = (own_num[i, :, s * ROW_BLOCK:(s + 1) * ROW_BLOCK, :].reshape(num_rows, head), stat_ref[pl.ds(h, 1), :], stat_ref[pl.ds(heads + h, 1), :])
-            theirs = (near_num[i, :, s * ROW_BLOCK:(s + 1) * ROW_BLOCK, :].reshape(num_rows, head), near_stat[pl.ds(h, 1), :], near_stat[pl.ds(heads + h, 1), :])
+            rows = slice(s * ROW_BLOCK, (s + 1) * ROW_BLOCK)
+            mine = (own_num[i, :, rows, :].reshape(num_rows, head), stat_ref[pl.ds(h, 1), :], stat_ref[pl.ds(heads + h, 1), :])
+            theirs = (near_num[i, :, rows, :].reshape(num_rows, head), near_stat[pl.ds(h, 1), :], near_stat[pl.ds(heads + h, 1), :])
             store(part.at[i, s], merge(mine, theirs))
+            if send is not None:
+                send(0, s).start()
 
     def long_copy(hop, s):
         i = 0 if hop == 0 else 2 * hop
@@ -362,17 +377,15 @@
 
     swap_stat.wait_recv()
     for hop in range(far):
-        own(2 * hop)
         if hop == 0:
-            for s in range(share):
-                long_copy(0, s).start()
-        own(2 * hop + 1)
-        if hop == 0:
-            for s in range(share):
-                short_copy(0, s).start()
+            own(0, long_copy)
+            own(1, short_copy)
+            start_swaps(4, nz)
             fetch_x.start()
             fetch_some(2)
             continue
+        own(2 * hop)
+        own(2 * hop + 1)
         for s in range(share):
             long_copy(hop - 1, s).wait_recv()
             store(part.at[2 * hop, s], merge(load(part.at[2 * hop, s]), load(from_long.at[hop - 1, s])))
@@ -518,6 +531,7 @@
             pltpu.VMEM((num_rows, width), BF16),
             pltpu.VMEM((nz, num_rows // ROW_BLOCK, share * ROW_BLOCK, head), F32),
             pltpu.VMEM((nz, num_rows // ROW_BLOCK, share * ROW_BLOCK, head), F32),
+            pltpu.VMEM((nz, num_rows // ROW_BLOCK, share * ROW_BLOCK, head), F32),
             pltpu.VMEM((2 * heads, num_rows), F32),
             pltpu.VMEM((nz, share) + piece, F32),
             pltpu.VMEM((far, share) + piece, F32),
@@ -528,7 +542,7 @@
             pltpu.VMEM((OUT_SLOTS, 2 * head, width), BF16),
             dma((1,)),
             dma((width // OUT_TILE,)),
-            dma((nz,)),
+            dma((2, nz)),
             dma((OUT_SLOTS, 2)),
             dma((2,)),
             dma((nz,)),

time: 85.9 us -> 83.6 us (0.973)
  Pallas kernels: 82.3 us -> 79.9 us
    pallas_call x1, Pallas kernels: 13.7 us -> 10.8 us  [attend(): pl.pallas_call(attend_kernel, name='attend', out_shape=(jax.ShapeDtypeStr...]
where the time goes in v5:
time: 83.6 us; the launch traced here: 83.3 us
  Pallas kernels  79.9 us (96%)
  local copies, waits for them, and re-layouts  2.69 us (3%)
    pallas_call x1, Pallas kernels, combine(): pl.pallas_call(functools.partial(combine_kernel, nz), name='combine', out...  47.1 us
    pallas_call x1, Pallas kernels, project(): pl.pallas_call(project_kernel, name='project', out_shape=(jax.ShapeDtypeS...  22.1 us
    pallas_call x1, Pallas kernels, attend(): pl.pallas_call(attend_kernel, name='attend', out_shape=(jax.ShapeDtypeStr...  10.8 us
    unnamed x1, local copies, waits for them, and re-layouts  2.69 us

profile of v5, /device:TPU:21, one launch (start us, length us, event | category | flops | bytes accessed | tf_op | source)
XLA Modules:
  0.0 83.3 jit_solution(6046070372766233028)
XLA Ops:
  0.6 22.1 %project.1 = (f32[16,384,128]{2,1,0:T(8,128)}, f32[128,128]{1,0:T(8,128)}, f32[128,128]{1,0:T(8,128)}) custom-call(f32[1,128]{1,0:T(1,128)} %constant.2.clone.freq_ref, s32[1,128]{1,0:T(1,128)} %bitcast.1, bf16[6144]{0:T(1024)(128)(2,1)} %w_norm_ref.1, bf16[128,6144]{1,0:T(8,128)(2,1)} %x_hbm.3, bf16[6144,6144]{1,0:T(8,128)(2,1)} %w_q_ref.1, ...), custom_call_target="tpu_custom_call" | custom-call | tf_op jit(solution)/shard_map/project/pallas_call | solution.py:137
  22.7 10.8 %attend.1 = (bf16[128,128,128]{2,1,0:T(8,128)(2,1)}, bf16[128,128,128]{2,1,0:T(8,128)(2,1)}, f32[16,384,128]{2,1,0:T(8,128)}, f32[96,128]{1,0:T(8,128)}) custom-call(s32[128]{0:T(128)} %len_ref.1, f32[128,128]{1,0:T(8,128)} %get-tuple-element.10.k_new_ref, f32[128,128]{1,0:T(8,128)} %get-tuple-element.11.v_new_ref, f32[16,384,128]{2,1,0:T(8,128)} %get-tuple-element.12.q_hbm, ...), custom_call_target="tpu_custom_call" | custom-call | tf_op jit(solution)/shard_map/attend/pallas_call | solution.py:241
  33.5 47.1 %combine.1 = bf16[128,6144]{1,0:T(8,128)(2,1)} custom-call(f32[96,128]{1,0:T(8,128)} %get-tuple-element.13.stat_ref, f32[16,384,128]{2,1,0:T(8,128)} %get-tuple-element.14.num_ref, bf16[128,6144]{1,0:T(8,128)(2,1)} %x_hbm.3, bf16[6144,6144]{1,0:T(8,128)(2,1)} %w_o_ref.1), custom_call_target="tpu_custom_call" | custom-call | tf_op jit(solution)/shard_map/combine/pallas_call | solution.py:523
  80.6 2.7 %copy.14 = bf16[128,6144]{1,0:T(8,128)(2,1)} copy(bf16[128,6144]{1,0:T(8,128)(2,1)} %combine.1) | data formatting | bytes 3145728

commit v6 on v5

--- a/solution.py
+++ b/solution.py
@@ -54,9 +54,8 @@
     fetch_v = pltpu.make_async_copy(w_v_ref, w_buf.at[0, :, pl.ds(head, head)], kv_sem.at[1])
     fetch_x = pltpu.make_async_copy(x_hbm, x_ref, x_sem.at[0])
     fetch_x.start()
-    fetch_k.start()
-    fetch_v.start()
     fetch(0).start()
+    fetch(1).start()
 
     gain = 1.0 + w_norm_ref[...].astype(F32)
     angles = jnp.broadcast_to(len_ref[...].astype(F32), (num_rows, num_rows)).T * freq_ref[...]
@@ -66,7 +65,7 @@
     cos_t = jnp.cos(angles)
     sin_t = jnp.where(lax.broadcasted_iota(jnp.int32, angles.shape, 1) < head // 2, -1.0, 1.0) * jnp.sin(angles)
     fetch_x.wait()
-    for block in range(1, PROJ_WINDOW):
+    for block in range(2, PROJ_WINDOW):
         fetch(block).start()
 
     def normalise(step, carry):
@@ -82,11 +81,6 @@
         u = u.astype(BF16).astype(F32)
         return u * cos_t + pltpu.roll(u, head // 2, 1) * sin_t
 
-    fetch_k.wait()
-    fetch_v.wait()
-    both = jnp.dot(x_norm[...], w_buf[0], preferred_element_type=F32)
-    k_ref[...] = rotate(both[:, :head]).astype(BF16).astype(F32)
-    v_ref[...] = both[:, head:].astype(BF16).astype(F32)
     enter([partner])
 
     def heads_of(c, block):
@@ -103,6 +97,11 @@
         @pl.when(block + PROJ_WINDOW < num_blocks)
         def _():
             fetch(block + PROJ_WINDOW).start()
+
+        @pl.when(block + PROJ_WINDOW == num_blocks)
+        def _():
+            fetch_k.start()
+            fetch_v.start()
 
         fetch(block).wait()
         product = jnp.dot(x_norm[...], w_buf[block + 1], preferred_element_type=F32)
@@ -114,6 +113,11 @@
         return carry
 
     lax.fori_loop(0, num_blocks, step, 0)
+    fetch_k.wait()
+    fetch_v.wait()
+    both = jnp.dot(x_norm[...], w_buf[0], preferred_element_type=F32)
+    k_ref[...] = rotate(both[:, :head]).astype(BF16).astype(F32)
+    v_ref[...] = both[:, head:].astype(BF16).astype(F32)
 
     def finish(block, carry):
         keep(block).wait()
@@ -172,10 +176,13 @@
         sem = in_sem.at[lax.rem(step, ATTEND_WINDOW + 1)]
         return [pltpu.make_async_copy(src, dst, sem) for src, dst in ((k_hbm.at[block], k_ref.at[block]), (v_hbm.at[block], v_ref.at[block]), (q_hbm.at[part], q_ref.at[part]))]
 
-    def stores(step):
+    def store_caches(step):
         block = pl.ds(step * rows, rows)
+        return [pltpu.make_async_copy(src, dst, out_sem.at[0]) for src, dst in ((k_ref.at[block], k_out_hbm.at[block]), (v_ref.at[block], v_out_hbm.at[block]))]
+
+    def store_partial(step):
         part = pl.ds(step * blocks, blocks)
-        return [pltpu.make_async_copy(src, dst, out_sem.at[0]) for src, dst in ((k_ref.at[block], k_out_hbm.at[block]), (v_ref.at[block], v_out_hbm.at[block]), (num_ref.at[part], num_hbm.at[part]))]
+        return pltpu.make_async_copy(num_ref.at[part], num_hbm.at[part], out_sem.at[0])
 
     def start(step, carry):
         for copy in loads(step):
@@ -185,12 +192,17 @@
     def attend_rows(step, carry):
         first = step * rows
 
+        for copy in loads(step):
+            copy.wait()
+
+        @pl.when(step == 0)
+        def _():
+            start(ATTEND_WINDOW - 1, 0)
+
         @pl.when(step + ATTEND_WINDOW < steps)
         def _():
             start(step + ATTEND_WINDOW, 0)
 
-        for copy in loads(step):
-            copy.wait()
         places = [len_ref[first + r] - base for r in range(rows)]
         for new, cache in ((k_new_ref, k_ref), (v_new_ref, v_ref)):
             fresh = new[pl.ds(pl.multiple_of(first, rows), rows), :]
@@ -202,6 +214,8 @@
             queries = q_ref.at[step * blocks + r // ROW_BLOCK]
             q = queries[pl.ds(r % ROW_BLOCK, heads, stride=ROW_BLOCK), :].astype(BF16)
             scores_ref[r] = lax.dot_general(q, k_ref[first + r], (((1,), (1,)), ((), ())), preferred_element_type=F32)
+        for copy in store_caches(step):
+            copy.start()
         stat_m = stat_ref[0:heads, :]
         stat_l = stat_ref[heads:2 * heads, :]
         for r, p in enumerate(places):
@@ -218,16 +232,16 @@
         for r in range(rows):
             partial = num_ref.at[step * blocks + r // ROW_BLOCK]
             partial[pl.ds(r % ROW_BLOCK, heads, stride=ROW_BLOCK), :] = jnp.dot(factors_ref[r], v_ref[first + r], preferred_element_type=F32)
-        for copy in stores(step):
-            copy.start()
+        store_partial(step).start()
         return carry
 
     def finish(step, carry):
-        for copy in stores(step):
+        for copy in store_caches(step):
             copy.wait()
+        store_partial(step).wait()
         return carry
 
-    lax.fori_loop(0, ATTEND_WINDOW, start, 0)
+    lax.fori_loop(0, ATTEND_WINDOW - 1, start, 0)
     lax.fori_loop(0, steps, attend_rows, 0)
     lax.fori_loop(0, steps, finish, 0)
 

time: 83.6 us -> 82.7 us (0.989)
    pallas_call x1, Pallas kernels: 22.1 us -> 21.1 us  [project(): pl.pallas_call(project_kernel, name='project', out_shape=(jax.ShapeDtypeS...]
where the time goes in v6:
time: 82.7 us; the launch traced here: 82.4 us
  Pallas kernels  79.1 us (96%)
  local copies, waits for them, and re-layouts  2.69 us (3%)
    pallas_call x1, Pallas kernels, combine(): pl.pallas_call(functools.partial(combine_kernel, nz), name='combine', out...  47.1 us
    pallas_call x1, Pallas kernels, project(): pl.pallas_call(project_kernel, name='project', out_shape=(jax.ShapeDtypeS...  21.1 us
    pallas_call x1, Pallas kernels, attend(): pl.pallas_call(attend_kernel, name='attend', out_shape=(jax.ShapeDtypeStr...  10.9 us
    unnamed x1, local copies, waits for them, and re-layouts  2.69 us

profile of v6, /device:TPU:21, one launch (start us, length us, event | category | flops | bytes accessed | tf_op | source)
XLA Modules:
  0.0 82.4 jit_solution(1313722955106155549)
XLA Ops:
  0.6 21.1 %project.1 = (f32[16,384,128]{2,1,0:T(8,128)}, f32[128,128]{1,0:T(8,128)}, f32[128,128]{1,0:T(8,128)}) custom-call(f32[1,128]{1,0:T(1,128)} %constant.2.clone.freq_ref, s32[1,128]{1,0:T(1,128)} %bitcast.1, bf16[6144]{0:T(1024)(128)(2,1)} %w_norm_ref.1, bf16[128,6144]{1,0:T(8,128)(2,1)} %x_hbm.3, bf16[6144,6144]{1,0:T(8,128)(2,1)} %w_q_ref.1, ...), custom_call_target="tpu_custom_call" | custom-call | tf_op jit(solution)/shard_map/project/pallas_call | solution.py:141
  21.7 10.9 %attend.1 = (bf16[128,128,128]{2,1,0:T(8,128)(2,1)}, bf16[128,128,128]{2,1,0:T(8,128)(2,1)}, f32[16,384,128]{2,1,0:T(8,128)}, f32[96,128]{1,0:T(8,128)}) custom-call(s32[128]{0:T(128)} %len_ref.1, f32[128,128]{1,0:T(8,128)} %get-tuple-element.10.k_new_ref, f32[128,128]{1,0:T(8,128)} %get-tuple-element.11.v_new_ref, f32[16,384,128]{2,1,0:T(8,128)} %get-tuple-element.12.q_hbm, ...), custom_call_target="tpu_custom_call" | custom-call | tf_op jit(solution)/shard_map/attend/pallas_call | solution.py:255
  32.7 47.1 %combine.1 = bf16[128,6144]{1,0:T(8,128)(2,1)} custom-call(f32[96,128]{1,0:T(8,128)} %get-tuple-element.13.stat_ref, f32[16,384,128]{2,1,0:T(8,128)} %get-tuple-element.14.num_ref, bf16[128,6144]{1,0:T(8,128)(2,1)} %x_hbm.3, bf16[6144,6144]{1,0:T(8,128)(2,1)} %w_o_ref.1), custom_call_target="tpu_custom_call" | custom-call | tf_op jit(solution)/shard_map/combine/pallas_call | solution.py:537
  79.7 2.7 %copy.14 = bf16[128,6144]{1,0:T(8,128)(2,1)} copy(bf16[128,6144]{1,0:T(8,128)(2,1)} %combine.1) | data formatting | bytes 3145728

commit v7 on v6

--- a/solution.py
+++ b/solution.py
@@ -450,6 +450,7 @@
         side_copy(0, s).start()
 
     tiles = width // OUT_TILE
+    start = me // (2 * nz)
 
     def save(n):
         columns = pl.ds(pl.multiple_of(n * OUT_TILE, OUT_TILE), OUT_TILE)
@@ -466,7 +467,7 @@
                 copy.wait()
 
         def tile(n, carry):
-            columns = pl.ds(pl.multiple_of(n * OUT_TILE, OUT_TILE), OUT_TILE)
+            columns = pl.ds(pl.multiple_of((start + n) * OUT_TILE, OUT_TILE), OUT_TILE)
             product = None
             for i, u in enumerate(us):
                 term = jnp.dot(attended[i], w_buf[u % OUT_SLOTS, :, columns], preferred_element_type=F32)
@@ -479,7 +480,8 @@
                 total[:, columns] = before + product
             return carry
 
-        lax.fori_loop(0, tiles, tile, 0)
+        for n in range(tiles):
+            tile(n, 0)
         for u in us:
             if u + OUT_SLOTS < len(units):
                 start_fetch(u + OUT_SLOTS)
@@ -492,6 +494,14 @@
     fetch_x.wait()
     multiply(chunks.pop(0))
     multiply(chunks.pop(0))
+    swap_stat.wait_send()
+    for swap in swaps:
+        swap.wait_send()
+    for s in range(share):
+        for hop in range(far):
+            long_copy(hop, s).wait_send()
+            if hop < far - 1:
+                short_copy(hop, s).wait_send()
     for hop in range(far):
         for s in range(share):
             far_arrival(hop, s).wait_recv()
@@ -509,15 +519,10 @@
     for n in range(tiles):
         save(n).wait()
 
-    swap_stat.wait_send()
-    for swap in swaps:
-        swap.wait_send()
     for s in range(share):
         for hop in range(far):
-            long_copy(hop, s).wait_send()
             far_copy(hop, s).wait_send()
             if hop < far - 1:
-                short_copy(hop, s).wait_send()
                 back_copy(hop, s).wait_send()
         for k in range(nz):
             side_copy(k, s).wait_send()

time: 82.7 us -> 82.5 us (level)
  no operation moved by 1% of the time
where the time goes in v7:
time: 82.5 us; the launch traced here: 82.2 us
  Pallas kernels  78.9 us (96%)
  local copies, waits for them, and re-layouts  2.69 us (3%)
    pallas_call x1, Pallas kernels, combine(): pl.pallas_call(functools.partial(combine_kernel, nz), name='combine', out...  46.8 us
    pallas_call x1, Pallas kernels, project(): pl.pallas_call(project_kernel, name='project', out_shape=(jax.ShapeDtypeS...  21.1 us
    pallas_call x1, Pallas kernels, attend(): pl.pallas_call(attend_kernel, name='attend', out_shape=(jax.ShapeDtypeStr...  10.9 us
    unnamed x1, local copies, waits for them, and re-layouts  2.69 us

profile of v7, /device:TPU:21, one launch (start us, length us, event | category | flops | bytes accessed | tf_op | source)
XLA Modules:
  0.0 82.2 jit_solution(6009627906142285856)
XLA Ops:
  0.6 21.1 %project.1 = (f32[16,384,128]{2,1,0:T(8,128)}, f32[128,128]{1,0:T(8,128)}, f32[128,128]{1,0:T(8,128)}) custom-call(f32[1,128]{1,0:T(1,128)} %constant.2.clone.freq_ref, s32[1,128]{1,0:T(1,128)} %bitcast.1, bf16[6144]{0:T(1024)(128)(2,1)} %w_norm_ref.1, bf16[128,6144]{1,0:T(8,128)(2,1)} %x_hbm.3, bf16[6144,6144]{1,0:T(8,128)(2,1)} %w_q_ref.1, ...), custom_call_target="tpu_custom_call" | custom-call | tf_op jit(solution)/shard_map/project/pallas_call | solution.py:141
  21.7 10.9 %attend.1 = (bf16[128,128,128]{2,1,0:T(8,128)(2,1)}, bf16[128,128,128]{2,1,0:T(8,128)(2,1)}, f32[16,384,128]{2,1,0:T(8,128)}, f32[96,128]{1,0:T(8,128)}) custom-call(s32[128]{0:T(128)} %len_ref.1, f32[128,128]{1,0:T(8,128)} %get-tuple-element.10.k_new_ref, f32[128,128]{1,0:T(8,128)} %get-tuple-element.11.v_new_ref, f32[16,384,128]{2,1,0:T(8,128)} %get-tuple-element.12.q_hbm, ...), custom_call_target="tpu_custom_call" | custom-call | tf_op jit(solution)/shard_map/attend/pallas_call | solution.py:255
  32.7 46.8 %combine.1 = bf16[128,6144]{1,0:T(8,128)(2,1)} custom-call(f32[96,128]{1,0:T(8,128)} %get-tuple-element.13.stat_ref, f32[16,384,128]{2,1,0:T(8,128)} %get-tuple-element.14.num_ref, bf16[128,6144]{1,0:T(8,128)(2,1)} %x_hbm.3, bf16[6144,6144]{1,0:T(8,128)(2,1)} %w_o_ref.1), custom_call_target="tpu_custom_call" | custom-call | tf_op jit(solution)/shard_map/combine/pallas_call | solution.py:542
  79.5 2.7 %copy.14 = bf16[128,6144]{1,0:T(8,128)(2,1)} copy(bf16[128,6144]{1,0:T(8,128)(2,1)} %combine.1) | data formatting | bytes 3145728
